TPU v7x, 256 devices: a whole 4x4x8 slice. The times are simulated.
256 devices in a mesh: gx: 4 (over y), gy: 16 (over z, core), gz: 4 (over x).
Axes of the slice: x: 4, y: 4, z: 8, core: 2. Of those that a mesh axis runs over, the one named last changes fastest.
Arguments:
- initial: float32 [256, 512, 1024], P('gx', 'gy', 'gz'), may hold values from -6 to 6
- right_side: float32 [256, 512, 1024], P('gx', 'gy', 'gz'), may hold values from -12 to 12
- shift_field: float32 [256, 512, 1024], P('gx', 'gy', 'gz'), may hold values from 0.5 to 8
Outputs:
- relaxed: float32 [256, 512, 1024], P('gx', 'gy', 'gz')
All inputs are finite; a program needn't handle non-finite values.
Results may differ from a plain program's by a relative error of at most 0.00002.
Values sent between devices are 32-bit elements; how exact they have to be, the bound alone decides.
No kernel may reach another device: no remote copies, remote signals or barrier semaphores. Data moves between devices by JAX's collectives and lax.ppermute only.
A program may use at most 128 MiB of HBM per device.

v0:
```python
import jax
import jax.numpy as jnp
from jax import lax
from jax.experimental import pallas as pl
from jax.experimental.pallas import tpu as pltpu
from jax.sharding import PartitionSpec as P


SWEEPS = 4
WIDE = 4
WEIGHT = 0.8
VMEM = pl.BlockSpec(memory_space=pltpu.VMEM)
HBM = pl.BlockSpec(memory_space=pltpu.HBM)
F32 = jnp.float32


def call(kernel, outs, operands, flops, scratch=(), limit=4, from_hbm=False, to_hbm=False):
    return pl.pallas_call(
        kernel,
        out_shape=[jax.ShapeDtypeStruct(s, F32) for s in outs],
        in_specs=[HBM if from_hbm else VMEM] * len(operands),
        out_specs=[HBM if to_hbm else VMEM] * len(outs),
        scratch_shapes=scratch,
        compiler_params=pltpu.CompilerParams(vmem_limit_bytes=limit * 2**20),
        cost_estimate=pl.CostEstimate(flops=flops, bytes_accessed=2**20, transcendentals=0),
    )(*operands)


def odd(axis):
    return lax.rem(lax.axis_index(axis), 2)


def swap(sent, axis):
    n = lax.axis_size(axis)
    near = [(i, i ^ 1) for i in range(n)]
    far = [(i, (i + (1 if i % 2 else -1)) % n) for i in range(n)]
    return lax.ppermute(sent[0], axis, near), lax.ppermute(sent[1], axis, far)


def iota(shape, dim):
    return lax.broadcasted_iota(jnp.int32, shape, dim)


def fold(first, second, low):
    row = iota(first.shape, 0)
    keep = jnp.where(low, row, 7 - row) < 4
    return jnp.where(keep, first, pltpu.roll(second, 4, 0))


def unfold(above, below):
    head = iota(above.shape, 0) < 4
    return jnp.where(head, above, below), pltpu.roll(jnp.where(head, below, above), 4, 0)


def pack_y(u, r, s, near, far, ends, sem):
    ny = u.shape[1]
    is_odd = odd("gy") == 1
    copies = []
    for a, ref in enumerate((u, r, s)):
        for e, row in enumerate((0, ny - 8)):
            copy = pltpu.make_async_copy(ref.at[:, row : row + 8, :], ends.at[a, e], sem.at[a, e])
            copy.start()
            copies.append(copy)
    for a in range(3):
        copies[2 * a].wait()
        copies[2 * a + 1].wait()
        for face, low in ((near, is_odd), (far, jnp.logical_not(is_odd))):
            end = jnp.where(low, 0, 1)

            def body(i, c, face=face, low=low, end=end, a=a):
                face[a, i] = fold(ends[a, end, 2 * i], ends[a, end, 2 * i + 1], low)
                return c

            lax.fori_loop(0, u.shape[0] // 2, body, 0, unroll=8)


def pack_x(u, r, s, near, far):
    nx = u.shape[0]
    is_odd = odd("gx") == 1
    for face, low in ((near, is_odd), (far, jnp.logical_not(is_odd))):
        put = 0
        for ref, layers in ((u, WIDE), (r, WIDE - 1), (s, WIDE - 1)):
            start = jnp.where(low, 0, nx - layers)
            for k in range(layers):
                face[put] = ref[start + k]
                put += 1


def pack_z(u, r, s, near, far):
    nx, ny, nz = u.shape
    block = iota((ny, 128), 1) // 4
    half = iota((ny, 128), 1) < 64
    is_odd = odd("gz") == 1
    for a, ref in enumerate((u, r, s)):

        def body(g, c, ref=ref, a=a):
            low = jnp.zeros((ny, 128), F32)
            high = low
            for j in range(32):
                x = g * 32 + j
                both = jnp.where(half, ref[x, :, 0:128], ref[x, :, nz - 128 : nz])
                both = pltpu.roll(both, 4 * j, 1) if j else both
                low = jnp.where(block == j, both, low)
                high = jnp.where(block == (j - 1) % 32, both, high)
            near[a, g] = jnp.where(is_odd, low, high)
            far[a, g] = jnp.where(is_odd, high, low)
            return c

        lax.fori_loop(0, nx // 32, body, 0)


def pack_yz(za, zb, near, far):
    ny = za.shape[2]
    is_odd = odd("gy") == 1
    for face, low in ((near, is_odd), (far, jnp.logical_not(is_odd))):
        rows = pl.ds(pl.multiple_of(jnp.where(low, 0, ny - 8), 8), 8)
        for a in range(3):
            for g in range(za.shape[1]):
                face[a, g] = fold(za[a, g, rows, :], zb[a, g, rows, :], low)


def weight(shift):
    return WEIGHT / (6.0 + shift)


def spread_z(high, low, j):
    tile = jnp.where(iota(high.shape, 1) // 4 == j, high, low)
    return pltpu.roll(tile, 128 - 4 * j, 1) if j else tile


def unpack_z(za, zb, s, tu, tr, tw, w):
    is_odd = odd("gz") == 1

    def weigh(i, c):
        w[i] = weight(s[i])
        return c

    lax.fori_loop(0, s.shape[0], weigh, 0, unroll=2)
    for a, out in enumerate((tu, tr, tw)):

        def body(g, c, a=a, out=out):
            one, two = za[a, g], zb[a, g]
            high, low = jnp.where(is_odd, two, one), jnp.where(is_odd, one, two)
            for j in range(32):
                tile = spread_z(high, low, j)
                out[g * 32 + j] = weight(tile) if a == 2 else tile
            return c

        lax.fori_loop(0, za.shape[1], body, 0)


def unpack_y(u_y, u_f, b_y, b_f, yu, yr, yw, tu, tr, tw):
    is_odd = odd("gy") == 1
    z_odd = odd("gz") == 1
    for a, out in enumerate((yu, yr, yw)):

        def body(i, c, a=a, out=out):
            one, two = u_y[a, i], u_f[a, i]
            above, below = jnp.where(is_odd, two, one), jnp.where(is_odd, one, two)
            first, second = unfold(above, below)
            out[2 * i] = weight(first) if a == 2 else first
            out[2 * i + 1] = weight(second) if a == 2 else second
            return c

        lax.fori_loop(0, u_y.shape[1], body, 0, unroll=4)
    for a, out in enumerate((tu, tr, tw)):
        for g in range(b_y.shape[1]):
            one, two = b_y[a, g], b_f[a, g]
            above, below = jnp.where(is_odd, two, one), jnp.where(is_odd, one, two)
            near, far = unfold(above, below)
            high, low = jnp.where(z_odd, far, near), jnp.where(z_odd, near, far)
            for j in range(32):
                tile = spread_z(high, low, j)
                out[g * 32 + j] = weight(tile) if a == 2 else tile


LAYERS = [(a, k) for a, n in enumerate((WIDE, WIDE - 1, WIDE - 1)) for k in range(n)]


def pack_edges(yu, yr, yw, tu, tr, tw, eu, er, ew, near, far):
    nx = yu.shape[0]
    is_odd = odd("gx") == 1
    lane = iota((8, 128), 1) // 8
    for face, low in ((near, is_odd), (far, jnp.logical_not(is_odd))):
        total = [jnp.zeros((8, 128), F32)] * 5
        for q, (a, k) in enumerate(LAYERS):
            layers = WIDE if a == 0 else WIDE - 1
            x = jnp.where(low, k, nx - layers + k)
            face[q] = (yu, yr, yw)[a][x]
            for t in range(5):
                tile = (tu, tr, tw)[a][x, 8 * t : 8 * t + 8, :] if t < 4 else (eu, er, ew)[a][x]
                total[t] = jnp.where(lane == q, pltpu.roll(tile, 8 * q + 4, 1), total[t])
        for t in range(6):
            face[len(LAYERS) + t // 2, :, 128 * (t % 2) : 128 * (t % 2) + 128] = total[min(t, 4)]


def stencil(below, here, above, r, w):
    n, m = here.shape
    beside = below + above
    beside = beside + (pltpu.roll(here, 1, 0) + pltpu.roll(here, n - 1, 0))
    beside = beside + (pltpu.roll(here, 1, 1) + pltpu.roll(here, m - 1, 1))
    return 0.2 * here + w * (r + beside)


def whole(x, main, y, t, e):
    left = jnp.concatenate([main[x], y[x]], 0)
    return jnp.concatenate([left, jnp.concatenate([t[x], e[x]], 0)], 1)


PLANES = 2


def centre(*refs):
    u0, r0, w0 = refs[0:4], refs[4:8], refs[8:12]
    out, ends = refs[12], refs[13:16]
    steps = refs[16:19]
    nx, ny, nz = u0[0].shape

    def plane(k, x):
        return whole(x, *u0) if k == 0 else steps[k - 1][x]

    def one(k, x):
        r, w = whole(x, *r0), whole(x, *w0)
        new = stencil(plane(k, x - 1), plane(k, x), plane(k, x + 1), r, w)
        if k == SWEEPS - 1:
            out[x] = new[:ny, :nz]
        else:
            steps[k][x] = new

    def planes(i):
        return [(k, 1 + PLANES * i - k * (PLANES + 1) + j) for k in range(SWEEPS) for j in range(PLANES)]

    def valid(k, x):
        return k + 1 <= x <= nx - 2 - k

    count = -(-(nx - 1 + (SWEEPS - 1) * (PLANES + 1)) // PLANES)
    full = [i for i in range(count) if all(valid(*p) for p in planes(i))]

    def peeled(i):
        for p in planes(i):
            if valid(*p):
                one(*p)

    for i in range(full[0]):
        peeled(i)

    def body(i, c):
        for p in planes(i):
            one(*p)
        return c

    lax.fori_loop(full[0], full[-1] + 1, body, 0)
    for i in range(full[-1] + 1, count):
        peeled(i)
    for k in range(SWEEPS - 1):
        lo, hi = k + 1, nx - 1 - k
        for j, x in enumerate((lo, lo + 1, hi - 2, hi - 1)):
            ends[k][j] = steps[k][x]


def tail(*refs):
    u0, r0, w0 = refs[0:4], refs[4:8], refs[8:12]
    body, ends = refs[12], refs[13:16]
    x_near, x_far, c_near, c_far = refs[16:20]
    out = refs[20]
    halo, last, sem = refs[21:24]
    steps = refs[24:27]
    nx, ny, nz = u0[0].shape
    wait = []
    copy = pltpu.make_async_copy(body.at[WIDE : nx - WIDE], out.at[WIDE : nx - WIDE], sem.at[0])
    copy.start()
    wait.append(copy)
    is_odd = odd("gx") == 1
    for side in (0, 1):
        flip = is_odd if side == 0 else jnp.logical_not(is_odd)
        for q, (a, k) in enumerate(LAYERS):
            main = jnp.where(flip, x_far[q], x_near[q])
            rows = jnp.where(flip, c_far[q], c_near[q])
            put = lambda v: weight(v) if a == 2 else v
            halo[side, q, :ny, :nz] = put(main)
            halo[side, q, ny:, :nz] = rows
            for t in range(5):
                at = (len(LAYERS) + t // 2, slice(None), slice(128 * (t % 2), 128 * (t % 2) + 128))
                tile = jnp.where(flip, c_far[at], c_near[at])
                halo[side, q, 8 * t : 8 * t + 8, nz:] = pltpu.roll(tile, 124 - 8 * q, 1)

    def start(a, x):
        layers = WIDE if a == 0 else WIDE - 1
        base = (0, WIDE, 2 * WIDE - 1)[a]
        if x >= nx:
            return halo[0, base + x - nx]
        if x < 0:
            return halo[1, base + layers + x]
        return whole(x, *(u0, r0, w0)[a])

    for side in (0, 1):

        def value(k, x):
            if k == 0:
                return start(0, x)
            lo, hi = k, nx - 1 - k
            for j, e in enumerate((lo, lo + 1, hi - 1, hi)):
                if x == e:
                    return ends[k - 1][j]
            return steps[k - 1][side, x - span(k)[0]]

        def span(k):
            if side == 0:
                return nx - k, nx + SWEEPS - k
            return k - SWEEPS, k

        for k in range(1, SWEEPS + 1):
            a, b = span(k)
            for x in range(a, b):
                new = stencil(value(k - 1, x - 1), value(k - 1, x), value(k - 1, x + 1), start(1, x), start(2, x))
                if k == SWEEPS:
                    last[side, x - a] = new[:ny, :nz]
                else:
                    steps[k - 1][side, x - a] = new
        a, b = span(SWEEPS)
        copy = pltpu.make_async_copy(last.at[side], out.at[a:b], sem.at[1 + side])
        copy.start()
        wait.append(copy)
    for copy in wait:
        copy.wait()


def shards(u, r, s):
    nx, ny, nz = u.shape
    cells = nx * ny * nz
    raw = (u, r, s)
    scratch = [pltpu.VMEM((3, 2, nx, 8, nz), F32), pltpu.SemaphoreType.DMA((3, 2))]
    fixed = [pltpu.with_memory_space_constraint(v, pltpu.HBM) for v in raw]
    sent = call(pack_y, [(3, nx // 2, 8, nz)] * 2, fixed, cells // 4, scratch, 8, from_hbm=True)
    y = swap(sent, "gy")
    sent = call(pack_z, [(3, nx // 32, ny, 128)] * 2, raw, cells)
    z = swap(sent, "gz")
    sent = call(pack_x, [(len(LAYERS), ny, nz)] * 2, raw, cells // 8)
    x = swap(sent, "gx")
    sent = call(pack_yz, [(3, nx // 32, 8, 128)] * 2, z, cells // 64)
    b = swap(sent, "gy")
    *t, w = call(unpack_z, [(nx, ny, 128)] * 3 + [u.shape], (*z, s), 8 * cells)
    rows = call(unpack_y, [(nx, 8, nz)] * 3 + [(nx, 8, 128)] * 3, (*y, *b), cells)
    yy, e = rows[:3], rows[3:]
    sent = call(pack_edges, [(len(LAYERS) + 3, 8, nz)] * 2, (*yy, *t, *e), cells // 8)
    c = swap(sent, "gx")
    parts = [v for a, m in enumerate((u, r, w)) for v in (m, yy[a], t[a], e[a])]
    block = (ny + 2 * WIDE, nz + 128)
    scratch = [pltpu.VMEM((nx,) + block, F32)] * 3
    body, *ends = call(centre, [u.shape] + [(4,) + block] * 3, parts, 60 * cells, scratch, 16)
    scratch = [
        pltpu.VMEM((2, len(LAYERS)) + block, F32),
        pltpu.VMEM((2, WIDE, ny, nz), F32),
        pltpu.SemaphoreType.DMA((3,)),
    ] + [pltpu.VMEM((2, SWEEPS) + block, F32)] * 3
    (out,) = call(tail, [u.shape], (*parts, body, *ends, *x, *c), 8 * cells, scratch, 8, to_hbm=True)
    return out


def solution(mesh):
    spec = P("gx", "gy", "gz")
    return jax.shard_map(shards, mesh=mesh, in_specs=(spec,) * 3, out_specs=spec, check_vma=False)
```

profile of v0, /device:TPU:1, one launch (start us, length us, event | category | flops | bytes accessed | tf_op | source)
XLA Modules:
  0.0 42.0 jit_solution(7330791947218081232)
XLA Ops:
  0.0 0.0 copy-start.1
  0.0 0.0 copy-start
  0.0 0.0 copy-start.2
  0.0 2.1 %shard_map.37 = (f32[3,32,8,256]{3,2,1,0:T(8,128)S(1)}, f32[3,32,8,256]{3,2,1,0:T(8,128)S(1)}) custom-call(f32[64,32,256]{2,1,0:T(8,128)} %refs_0_.3, f32[64,32,256]{2,1,0:T(8,128)} %refs_4_.3, f32[64,32,256]{2,1,0:T(8,128)} %s.7), custom_call_target="tpu_custom_call" | custom-call | flops 131072 | bytes 1048576 | tf_op jit(solution)/shard_map/pallas_call | solution.py:18
  2.1 3.3 %collective-permute-start = (f32[3,32,8,256]{3,2,1,0:T(8,128)S(1)}, f32[3,32,8,256]{3,2,1,0:T(8,128)S(1)}, u32[]{:S(2)}, u32[]{:S(2)}) collective-permute-start(f32[3,32,8,256]{3,2,1,0:T(8,128)S(1)} %get-tuple-element.29), channel_id=1, source_target_pairs={{0,4},{4,0},{8,12},{12,8},{16,20},{20,16},{24,28},{28,24},{32,36},... | collective-permute-start | bytes 2359304 | tf_op jit(solution)/shard_map/ppermute | solution.py:37
  5.4 0.0 collective-permute-start.1
  5.4 0.0 copy-done.1
  5.4 0.0 copy-done
  5.4 0.0 copy-done.2
  5.5 1.2 %shard_map.38 = (f32[3,2,32,128]{3,2,1,0:T(8,128)S(1)}, f32[3,2,32,128]{3,2,1,0:T(8,128)S(1)}) custom-call(f32[64,32,256]{2,1,0:T(8,128)S(1)} %copy-done, f32[64,32,256]{2,1,0:T(8,128)S(1)} %copy-done.1, f32[64,32,256]{2,1,0:T(8,128)S(1)} %copy-done.2), custom_call_target="tpu_custom_call" | custom-call | flops 524288 | bytes 1048576 | tf_op jit(solution)/shard_map/pallas_call | solution.py:18
  6.7 1.2 %collective-permute-start.2 = (f32[3,2,32,128]{3,2,1,0:T(8,128)S(1)}, f32[3,2,32,128]{3,2,1,0:T(8,128)S(1)}, u32[]{:S(2)}, u32[]{:S(2)}) collective-permute-start(f32[3,2,32,128]{3,2,1,0:T(8,128)S(1)} %get-tuple-element.31), channel_id=1, source_target_pairs={{0,1},{1,0},{2,3},{3,2},{4,5},{5,4},{6,7},{7,6},{8,9},{9,8},{10,11... | collective-permute-start | bytes 294920 | tf_op jit(solution)/shard_map/ppermute | solution.py:37
  8.0 1.4 %collective-permute-start.6 = (f32[10,32,256]{2,1,0:T(8,128)S(1)}, f32[10,32,256]{2,1,0:T(8,128)S(1)}, u32[]{:S(2)}, u32[]{:S(2)}) collective-permute-start(f32[10,32,256]{2,1,0:T(8,128)S(1)} %get-tuple-element.49), channel_id=1, source_target_pairs={{0,64},{64,0},{128,192},{192,128},{1,65},{65,1},{129,193},{193,129... | collective-permute-start | bytes 983048 | tf_op jit(solution)/shard_map/ppermute | solution.py:37
  9.3 1.9 %collective-permute-start.7 = (f32[10,32,256]{2,1,0:T(8,128)S(1)}, f32[10,32,256]{2,1,0:T(8,128)S(1)}, u32[]{:S(2)}, u32[]{:S(2)}) collective-permute-start(f32[10,32,256]{2,1,0:T(8,128)S(1)} %get-tuple-element.50), channel_id=1, source_target_pairs={{0,192},{64,128},{128,64},{192,0},{1,193},{65,129},{129,65},{193,1... | collective-permute-start | bytes 983048 | tf_op jit(solution)/shard_map/ppermute | solution.py:37
  11.2 0.0 collective-permute-done.2.za
  11.2 1.8 %collective-permute-start.3 = (f32[3,2,32,128]{3,2,1,0:T(8,128)S(1)}, f32[3,2,32,128]{3,2,1,0:T(8,128)S(1)}, u32[]{:S(2)}, u32[]{:S(2)}) collective-permute-start(f32[3,2,32,128]{3,2,1,0:T(8,128)S(1)} %get-tuple-element.32), channel_id=1, source_target_pairs={{0,3},{1,2},{2,1},{3,0},{4,7},{5,6},{6,5},{7,4},{8,11},{9,10},{10,... | collective-permute-start | bytes 294920 | tf_op jit(solution)/shard_map/ppermute | solution.py:37
  13.1 3.2 %collective-permute-done.3.zb = f32[3,2,32,128]{3,2,1,0:T(8,128)S(1)} collective-permute-done((f32[3,2,32,128]{3,2,1,0:T(8,128)S(1)}, f32[3,2,32,128]{3,2,1,0:T(8,128)S(1)}, u32[]{:S(2)}, u32[]{:S(2)}) %collective-permute-start.3) | collective-permute-done | bytes 98336 | tf_op jit(solution)/shard_map/ppermute | solution.py:37
  16.2 6.1 %collective-permute-start.4 = (f32[3,2,8,128]{3,2,1,0:T(8,128)S(1)}, f32[3,2,8,128]{3,2,1,0:T(8,128)S(1)}, u32[]{:S(2)}, u32[]{:S(2)}) collective-permute-start(f32[3,2,8,128]{3,2,1,0:T(8,128)S(1)} %get-tuple-element.33), channel_id=1, source_target_pairs={{0,4},{4,0},{8,12},{12,8},{16,20},{20,16},{24,28},{28,24},{32,36},... | collective-permute-start | bytes 73736 | tf_op jit(solution)/shard_map/ppermute | solution.py:37
  22.4 0.8 %collective-permute-done.4.b_y = f32[3,2,8,128]{3,2,1,0:T(8,128)S(1)} collective-permute-done((f32[3,2,8,128]{3,2,1,0:T(8,128)S(1)}, f32[3,2,8,128]{3,2,1,0:T(8,128)S(1)}, u32[]{:S(2)}, u32[]{:S(2)}) %collective-permute-start.4) | collective-permute-done | bytes 24608 | tf_op jit(solution)/shard_map/ppermute | solution.py:37
  23.2 0.0 collective-permute-start.5
  23.2 1.8 %shard_map.41 = (f32[64,32,128]{2,1,0:T(8,128)S(1)}, f32[64,32,128]{2,1,0:T(8,128)S(1)}, f32[64,32,128]{2,1,0:T(8,128)S(1)}, f32[64,32,256]{2,1,0:T(8,128)S(1)}) custom-call(f32[3,2,32,128]{3,2,1,0:T(8,128)S(1)} %collective-permute-done.2.za, f32[3,2,32,128]{3,2,1,0:T(8,128)S(1)} %collective-permute-done.3.zb, f32[64,32,256]{2,1,0:T(8,128)S(1)} %copy-done.2), custom_call_target="tpu_custom_call" | custom-call | flops 4194304 | bytes 1048576 | tf_op jit(solution)/shard_map/pallas_call | solution.py:18
  25.0 1.5 %collective-permute-done.5.b_f = f32[3,2,8,128]{3,2,1,0:T(8,128)S(1)} collective-permute-done((f32[3,2,8,128]{3,2,1,0:T(8,128)S(1)}, f32[3,2,8,128]{3,2,1,0:T(8,128)S(1)}, u32[]{:S(2)}, u32[]{:S(2)}) %collective-permute-start.5) | collective-permute-done | bytes 24608 | tf_op jit(solution)/shard_map/ppermute | solution.py:37
  26.5 0.0 collective-permute-done.u_y
  26.5 0.0 collective-permute-done.1.u_f
  26.5 0.6 %shard_map.40 = (f32[64,8,256]{2,1,0:T(8,128)S(1)}, f32[64,8,256]{2,1,0:T(8,128)S(1)}, f32[64,8,256]{2,1,0:T(8,128)S(1)}, f32[64,8,128]{2,1,0:T(8,128)S(1)}, f32...) custom-call(f32[3,32,8,256]{3,2,1,0:T(8,128)S(1)} %collective-permute-done.u_y, ...), custom_call_target="tpu_custom_call" | custom-call | flops 524288 | bytes 1048576 | tf_op jit(solution)/shard_map/pallas_call | solution.py:18
  27.1 0.2 shard_map.44
  27.3 0.6 %collective-permute-start.8 = (f32[13,8,256]{2,1,0:T(8,128)S(1)}, f32[13,8,256]{2,1,0:T(8,128)S(1)}, u32[]{:S(2)}, u32[]{:S(2)}) collective-permute-start(f32[13,8,256]{2,1,0:T(8,128)S(1)} %get-tuple-element.51), channel_id=1, source_target_pairs={{0,64},{64,0},{128,192},{192,128},{1,65},{65,1},{129,193},{193,129... | collective-permute-start | bytes 319496 | tf_op jit(solution)/shard_map/ppermute | solution.py:37
  27.9 1.9 %collective-permute-start.9 = (f32[13,8,256]{2,1,0:T(8,128)S(1)}, f32[13,8,256]{2,1,0:T(8,128)S(1)}, u32[]{:S(2)}, u32[]{:S(2)}) collective-permute-start(f32[13,8,256]{2,1,0:T(8,128)S(1)} %get-tuple-element.52), channel_id=1, source_target_pairs={{0,192},{64,128},{128,64},{192,0},{1,193},{65,129},{129,65},{193,1... | collective-permute-start | bytes 319496 | tf_op jit(solution)/shard_map/ppermute | solution.py:37
  29.8 9.9 %shard_map.42 = (f32[64,32,256]{2,1,0:T(8,128)S(1)}, f32[4,40,384]{2,1,0:T(8,128)S(1)}, f32[4,40,384]{2,1,0:T(8,128)S(1)}, f32[4,40,384]{2,1,0:T(8,128)S(1)}) custom-call(f32[64,32,256]{2,1,0:T(8,128)S(1)} %copy-done, f32[64,8,256]{2,1,0:T(8,128)S(1)} %get-tuple-element.35.refs_1_.yu, f32[64,32,128]{2,1,0:T(8,128)S(1)} %get-tuple-element.36.refs_2_.tu, ...), custom_call_target="tpu_custom_call" | custom-call | flops 31457280 | bytes 1048576 | tf_op jit(solution)/shard_map/pallas_call | solution.py:18
  39.7 0.0 collective-permute-done.6.refs_16_
  39.7 0.0 collective-permute-done.7.refs_17_
  39.7 0.0 collective-permute-done.8.refs_18_
  39.7 0.0 collective-permute-done.9.refs_19_
  39.7 2.3 %shard_map.45 = f32[64,32,256]{2,1,0:T(8,128)} custom-call(f32[64,32,256]{2,1,0:T(8,128)S(1)} %copy-done, f32[64,8,256]{2,1,0:T(8,128)S(1)} %get-tuple-element.35.refs_1_.yu, f32[64,32,128]{2,1,0:T(8,128)S(1)} %get-tuple-element.36.refs_2_.tu, f32[64,8,128]{2,1,0:T(8,128)S(1)} %get-tuple-element.37.refs_3_.eu, f32[64,32,256]{2,1,0:T(8,128)S(1)} %copy-done.1, ...), custom_call_target="tpu_custom_call" | custom-call | flops 4194304 | bytes 1048576 | tf_op jit(solution)/shard_map/pallas_call | solution.py:18
  (2 shorter events, 0.1 us)
Async XLA Ops:
  0.0 5.4 %copy-start.1 = (f32[64,32,256]{2,1,0:T(8,128)S(1)}, f32[64,32,256]{2,1,0:T(8,128)}, u32[]{:S(2)}) copy-start(f32[64,32,256]{2,1,0:T(8,128)} %refs_4_.3) | copy-start | bytes 6291460
  0.0 5.4 %copy-start = (f32[64,32,256]{2,1,0:T(8,128)S(1)}, f32[64,32,256]{2,1,0:T(8,128)}, u32[]{:S(2)}) copy-start(f32[64,32,256]{2,1,0:T(8,128)} %refs_0_.3) | copy-start | bytes 6291460
  0.0 5.4 %copy-start.2 = (f32[64,32,256]{2,1,0:T(8,128)S(1)}, f32[64,32,256]{2,1,0:T(8,128)}, u32[]{:S(2)}) copy-start(f32[64,32,256]{2,1,0:T(8,128)} %s.7) | copy-start | bytes 6291460
  2.1 24.3 %collective-permute-start = (f32[3,32,8,256]{3,2,1,0:T(8,128)S(1)}, f32[3,32,8,256]{3,2,1,0:T(8,128)S(1)}, u32[]{:S(2)}, u32[]{:S(2)}) collective-permute-start(f32[3,32,8,256]{3,2,1,0:T(8,128)S(1)} %get-tuple-element.29), channel_id=1, source_target_pairs={{0,4},{4,0},{8,12},{12,8},{16,20},{20,16},{24,28},{28,24},{32,36},... | collective-permute-start | bytes 2359304 | tf_op jit(solution)/shard_map/ppermute | solution.py:37
  5.4 21.0 %collective-permute-start.1 = (f32[3,32,8,256]{3,2,1,0:T(8,128)S(1)}, f32[3,32,8,256]{3,2,1,0:T(8,128)S(1)}, u32[]{:S(2)}, u32[]{:S(2)}) collective-permute-start(f32[3,32,8,256]{3,2,1,0:T(8,128)S(1)} %get-tuple-element.30), channel_id=1, source_target_pairs={{0,60},{4,8},{8,4},{12,16},{16,12},{20,24},{24,20},{28,32},{32,28}... | collective-permute-start | bytes 2359304 | tf_op jit(solution)/shard_map/ppermute | solution.py:37
  6.7 4.5 %collective-permute-start.2 = (f32[3,2,32,128]{3,2,1,0:T(8,128)S(1)}, f32[3,2,32,128]{3,2,1,0:T(8,128)S(1)}, u32[]{:S(2)}, u32[]{:S(2)}) collective-permute-start(f32[3,2,32,128]{3,2,1,0:T(8,128)S(1)} %get-tuple-element.31), channel_id=1, source_target_pairs={{0,1},{1,0},{2,3},{3,2},{4,5},{5,4},{6,7},{7,6},{8,9},{9,8},{10,11... | collective-permute-start | bytes 294920 | tf_op jit(solution)/shard_map/ppermute | solution.py:37
  8.0 31.8 %collective-permute-start.6 = (f32[10,32,256]{2,1,0:T(8,128)S(1)}, f32[10,32,256]{2,1,0:T(8,128)S(1)}, u32[]{:S(2)}, u32[]{:S(2)}) collective-permute-start(f32[10,32,256]{2,1,0:T(8,128)S(1)} %get-tuple-element.49), channel_id=1, source_target_pairs={{0,64},{64,0},{128,192},{192,128},{1,65},{65,1},{129,193},{193,129... | collective-permute-start | bytes 983048 | tf_op jit(solution)/shard_map/ppermute | solution.py:37
  9.3 30.4 %collective-permute-start.7 = (f32[10,32,256]{2,1,0:T(8,128)S(1)}, f32[10,32,256]{2,1,0:T(8,128)S(1)}, u32[]{:S(2)}, u32[]{:S(2)}) collective-permute-start(f32[10,32,256]{2,1,0:T(8,128)S(1)} %get-tuple-element.50), channel_id=1, source_target_pairs={{0,192},{64,128},{128,64},{192,0},{1,193},{65,129},{129,65},{193,1... | collective-permute-start | bytes 983048 | tf_op jit(solution)/shard_map/ppermute | solution.py:37
  11.2 5.0 %collective-permute-start.3 = (f32[3,2,32,128]{3,2,1,0:T(8,128)S(1)}, f32[3,2,32,128]{3,2,1,0:T(8,128)S(1)}, u32[]{:S(2)}, u32[]{:S(2)}) collective-permute-start(f32[3,2,32,128]{3,2,1,0:T(8,128)S(1)} %get-tuple-element.32), channel_id=1, source_target_pairs={{0,3},{1,2},{2,1},{3,0},{4,7},{5,6},{6,5},{7,4},{8,11},{9,10},{10,... | collective-permute-start | bytes 294920 | tf_op jit(solution)/shard_map/ppermute | solution.py:37
  16.2 7.0 %collective-permute-start.4 = (f32[3,2,8,128]{3,2,1,0:T(8,128)S(1)}, f32[3,2,8,128]{3,2,1,0:T(8,128)S(1)}, u32[]{:S(2)}, u32[]{:S(2)}) collective-permute-start(f32[3,2,8,128]{3,2,1,0:T(8,128)S(1)} %get-tuple-element.33), channel_id=1, source_target_pairs={{0,4},{4,0},{8,12},{12,8},{16,20},{20,16},{24,28},{28,24},{32,36},... | collective-permute-start | bytes 73736 | tf_op jit(solution)/shard_map/ppermute | solution.py:37
  23.2 3.3 %collective-permute-start.5 = (f32[3,2,8,128]{3,2,1,0:T(8,128)S(1)}, f32[3,2,8,128]{3,2,1,0:T(8,128)S(1)}, u32[]{:S(2)}, u32[]{:S(2)}) collective-permute-start(f32[3,2,8,128]{3,2,1,0:T(8,128)S(1)} %get-tuple-element.34), channel_id=1, source_target_pairs={{0,60},{4,8},{8,4},{12,16},{16,12},{20,24},{24,20},{28,32},{32,28}... | collective-permute-start | bytes 73736 | tf_op jit(solution)/shard_map/ppermute | solution.py:37
  27.3 12.5 %collective-permute-start.8 = (f32[13,8,256]{2,1,0:T(8,128)S(1)}, f32[13,8,256]{2,1,0:T(8,128)S(1)}, u32[]{:S(2)}, u32[]{:S(2)}) collective-permute-start(f32[13,8,256]{2,1,0:T(8,128)S(1)} %get-tuple-element.51), channel_id=1, source_target_pairs={{0,64},{64,0},{128,192},{192,128},{1,65},{65,1},{129,193},{193,129... | collective-permute-start | bytes 319496 | tf_op jit(solution)/shard_map/ppermute | solution.py:37
  27.9 11.8 %collective-permute-start.9 = (f32[13,8,256]{2,1,0:T(8,128)S(1)}, f32[13,8,256]{2,1,0:T(8,128)S(1)}, u32[]{:S(2)}, u32[]{:S(2)}) collective-permute-start(f32[13,8,256]{2,1,0:T(8,128)S(1)} %get-tuple-element.52), channel_id=1, source_target_pairs={{0,192},{64,128},{128,64},{192,0},{1,193},{65,129},{129,65},{193,1... | collective-permute-start | bytes 319496 | tf_op jit(solution)/shard_map/ppermute | solution.py:37
where the time goes:
time: 42.7 us; the launch traced here: 42 us
  Pallas kernels  18.2 us (43%)
  starting transfers between devices  18.2 us (43%)
  waiting for transfers between devices  5.48 us (13%)
    ppermute x10, starting transfers between devices, swap(): return (lax.ppermute(sent[0], axis, near), lax.ppermute(sent[1], axis, far))  18.2 us
    pallas_call x9, Pallas kernels, call(): pl.pallas_call(kernel, out_shape=[jax.ShapeDtypeStruct(s, F32) for s in o...  18.2 us
    ppermute x10, waiting for transfers between devices, swap(): return (lax.ppermute(sent[0], axis, near), lax.ppermute(sent[1], axis, far))  5.48 us
  transfers between devices with their start and end apart: 10, of which 3 were waited for; matrix products, arithmetic and copies ran while one was open for 0% of the time, Pallas kernels for 33%

commit v1 on v0

--- a/solution.py
+++ b/solution.py
@@ -12,15 +12,17 @@
 VMEM = pl.BlockSpec(memory_space=pltpu.VMEM)
 HBM = pl.BlockSpec(memory_space=pltpu.HBM)
 F32 = jnp.float32
-
-
-def call(kernel, outs, operands, flops, scratch=(), limit=4, from_hbm=False, to_hbm=False):
+LAYERS = [(a, k) for a, n in enumerate((WIDE, WIDE - 1, WIDE - 1)) for k in range(n)]
+
+
+def call(kernel, outs, operands, flops, scratch=(), limit=4, hbm_in=(), hbm_out=(), aliases={}):
     return pl.pallas_call(
         kernel,
         out_shape=[jax.ShapeDtypeStruct(s, F32) for s in outs],
-        in_specs=[HBM if from_hbm else VMEM] * len(operands),
-        out_specs=[HBM if to_hbm else VMEM] * len(outs),
+        in_specs=[HBM if i in hbm_in else VMEM for i in range(len(operands))],
+        out_specs=[HBM if i in hbm_out else VMEM for i in range(len(outs))],
         scratch_shapes=scratch,
+        input_output_aliases=aliases,
         compiler_params=pltpu.CompilerParams(vmem_limit_bytes=limit * 2**20),
         cost_estimate=pl.CostEstimate(flops=flops, bytes_accessed=2**20, transcendentals=0),
     )(*operands)
@@ -128,14 +130,16 @@
     return pltpu.roll(tile, 128 - 4 * j, 1) if j else tile
 
 
-def unpack_z(za, zb, s, tu, tr, tw, w):
-    is_odd = odd("gz") == 1
-
-    def weigh(i, c):
+def weigh(s, w):
+    def body(i, c):
         w[i] = weight(s[i])
         return c
 
-    lax.fori_loop(0, s.shape[0], weigh, 0, unroll=2)
+    lax.fori_loop(0, s.shape[0], body, 0, unroll=2)
+
+
+def unpack_z(za, zb, tu, tr, tw):
+    is_odd = odd("gz") == 1
     for a, out in enumerate((tu, tr, tw)):
 
         def body(g, c, a=a, out=out):
@@ -149,39 +153,35 @@
         lax.fori_loop(0, za.shape[1], body, 0)
 
 
-def unpack_y(u_y, u_f, b_y, b_f, yu, yr, yw, tu, tr, tw):
+def unpack_y(near, far, yu, yr, yw):
     is_odd = odd("gy") == 1
-    z_odd = odd("gz") == 1
     for a, out in enumerate((yu, yr, yw)):
 
         def body(i, c, a=a, out=out):
-            one, two = u_y[a, i], u_f[a, i]
+            one, two = near[a, i], far[a, i]
             above, below = jnp.where(is_odd, two, one), jnp.where(is_odd, one, two)
             first, second = unfold(above, below)
             out[2 * i] = weight(first) if a == 2 else first
             out[2 * i + 1] = weight(second) if a == 2 else second
             return c
 
-        lax.fori_loop(0, u_y.shape[1], body, 0, unroll=4)
-    for a, out in enumerate((tu, tr, tw)):
-        for g in range(b_y.shape[1]):
-            one, two = b_y[a, g], b_f[a, g]
-            above, below = jnp.where(is_odd, two, one), jnp.where(is_odd, one, two)
-            near, far = unfold(above, below)
-            high, low = jnp.where(z_odd, far, near), jnp.where(z_odd, near, far)
+        lax.fori_loop(0, near.shape[1], body, 0, unroll=4)
+
+
+def pack_edges(b_near, b_far, yu, yr, yw, tu, tr, tw, eu, er, ew, near, far):
+    y_odd, z_odd, x_odd = odd("gy") == 1, odd("gz") == 1, odd("gx") == 1
+    for a, out in enumerate((eu, er, ew)):
+        for g in range(b_near.shape[1]):
+            one, two = b_near[a, g], b_far[a, g]
+            above, below = jnp.where(y_odd, two, one), jnp.where(y_odd, one, two)
+            first, second = unfold(above, below)
+            high, low = jnp.where(z_odd, second, first), jnp.where(z_odd, first, second)
             for j in range(32):
                 tile = spread_z(high, low, j)
                 out[g * 32 + j] = weight(tile) if a == 2 else tile
-
-
-LAYERS = [(a, k) for a, n in enumerate((WIDE, WIDE - 1, WIDE - 1)) for k in range(n)]
-
-
-def pack_edges(yu, yr, yw, tu, tr, tw, eu, er, ew, near, far):
     nx = yu.shape[0]
-    is_odd = odd("gx") == 1
     lane = iota((8, 128), 1) // 8
-    for face, low in ((near, is_odd), (far, jnp.logical_not(is_odd))):
+    for face, low in ((near, x_odd), (far, jnp.logical_not(x_odd))):
         total = [jnp.zeros((8, 128), F32)] * 5
         for q, (a, k) in enumerate(LAYERS):
             layers = WIDE if a == 0 else WIDE - 1
@@ -210,11 +210,29 @@
 PLANES = 2
 
 
+def planes(i):
+    return [(k, 1 + PLANES * i - k * (PLANES + 1) + j) for k in range(SWEEPS) for j in range(PLANES)]
+
+
+def steps_of(nx):
+    def valid(k, x):
+        return k + 1 <= x <= nx - 2 - k
+
+    count = -(-(nx - 1 + (SWEEPS - 1) * (PLANES + 1)) // PLANES)
+    done = [[p for p in planes(i) if valid(*p)] for i in range(count)]
+    full = [i for i in range(count) if len(done[i]) == SWEEPS * PLANES]
+    first = planes(full[0])[-PLANES][1]
+    stop = planes(full[-1])[-1][1] + 1
+    return done, full, first, stop
+
+
 def centre(*refs):
     u0, r0, w0 = refs[0:4], refs[4:8], refs[8:12]
-    out, ends = refs[12], refs[13:16]
-    steps = refs[16:19]
+    out, rest, ends = refs[12], refs[13], refs[14:17]
+    last, sem = refs[17:19]
+    steps = refs[19:22]
     nx, ny, nz = u0[0].shape
+    done, full, first, stop = steps_of(nx)
 
     def plane(k, x):
         return whole(x, *u0) if k == 0 else steps[k - 1][x]
@@ -222,54 +240,50 @@
     def one(k, x):
         r, w = whole(x, *r0), whole(x, *w0)
         new = stencil(plane(k, x - 1), plane(k, x), plane(k, x + 1), r, w)
-        if k == SWEEPS - 1:
-            out[x] = new[:ny, :nz]
+        if k < SWEEPS - 1:
+            steps[k][x] = new
+        elif isinstance(x, int):
+            rest[x - stop if x >= stop else nx - WIDE - stop + x - WIDE] = new[:ny, :nz]
         else:
-            steps[k][x] = new
-
-    def planes(i):
-        return [(k, 1 + PLANES * i - k * (PLANES + 1) + j) for k in range(SWEEPS) for j in range(PLANES)]
-
-    def valid(k, x):
-        return k + 1 <= x <= nx - 2 - k
-
-    count = -(-(nx - 1 + (SWEEPS - 1) * (PLANES + 1)) // PLANES)
-    full = [i for i in range(count) if all(valid(*p) for p in planes(i))]
-
-    def peeled(i):
-        for p in planes(i):
-            if valid(*p):
-                one(*p)
+            last[x] = new[:ny, :nz]
 
     for i in range(full[0]):
-        peeled(i)
+        for p in done[i]:
+            one(*p)
 
     def body(i, c):
         for p in planes(i):
             one(*p)
+        at = pl.ds(planes(i)[-PLANES][1], PLANES)
+        pltpu.make_async_copy(last.at[at], out.at[at], sem).start()
         return c
 
     lax.fori_loop(full[0], full[-1] + 1, body, 0)
-    for i in range(full[-1] + 1, count):
-        peeled(i)
+    for i in range(full[-1] + 1, len(done)):
+        for p in done[i]:
+            one(*p)
     for k in range(SWEEPS - 1):
         lo, hi = k + 1, nx - 1 - k
         for j, x in enumerate((lo, lo + 1, hi - 2, hi - 1)):
             ends[k][j] = steps[k][x]
+    pltpu.make_async_copy(last.at[first:stop], out.at[first:stop], sem).wait()
 
 
 def tail(*refs):
     u0, r0, w0 = refs[0:4], refs[4:8], refs[8:12]
-    body, ends = refs[12], refs[13:16]
-    x_near, x_far, c_near, c_far = refs[16:20]
-    out = refs[20]
-    halo, last, sem = refs[21:24]
-    steps = refs[24:27]
+    rest, ends = refs[13], refs[14:17]
+    x_near, x_far, c_near, c_far = refs[17:21]
+    out = refs[21]
+    halo, last, sem = refs[22:25]
+    steps = refs[25:28]
     nx, ny, nz = u0[0].shape
+    _, _, first, stop = steps_of(nx)
     wait = []
-    copy = pltpu.make_async_copy(body.at[WIDE : nx - WIDE], out.at[WIDE : nx - WIDE], sem.at[0])
-    copy.start()
-    wait.append(copy)
+    if first > WIDE:
+        wait.append(pltpu.make_async_copy(rest.at[nx - WIDE - stop :], out.at[WIDE:first], sem.at[2]))
+    wait.append(pltpu.make_async_copy(rest.at[: nx - WIDE - stop], out.at[stop : nx - WIDE], sem.at[3]))
+    for copy in wait:
+        copy.start()
     is_odd = odd("gx") == 1
     for side in (0, 1):
         flip = is_odd if side == 0 else jnp.logical_not(is_odd)
@@ -293,32 +307,30 @@
             return halo[1, base + layers + x]
         return whole(x, *(u0, r0, w0)[a])
 
+    def span(side, k):
+        return (nx - k, nx + SWEEPS - k) if side == 0 else (k - SWEEPS, k)
+
+    def value(side, k, x):
+        if k == 0:
+            return start(0, x)
+        for j, e in enumerate((k, k + 1, nx - 2 - k, nx - 1 - k)):
+            if x == e:
+                return ends[k - 1][j]
+        return steps[k - 1][side, x - span(side, k)[0]]
+
+    for k in range(1, SWEEPS + 1):
+        for j in range(SWEEPS):
+            for side in (0, 1):
+                x = span(side, k)[0] + j
+                near = [value(side, k - 1, x + d) for d in (-1, 0, 1)]
+                new = stencil(*near, start(1, x), start(2, x))
+                if k == SWEEPS:
+                    last[side, j] = new[:ny, :nz]
+                else:
+                    steps[k - 1][side, j] = new
     for side in (0, 1):
-
-        def value(k, x):
-            if k == 0:
-                return start(0, x)
-            lo, hi = k, nx - 1 - k
-            for j, e in enumerate((lo, lo + 1, hi - 1, hi)):
-                if x == e:
-                    return ends[k - 1][j]
-            return steps[k - 1][side, x - span(k)[0]]
-
-        def span(k):
-            if side == 0:
-                return nx - k, nx + SWEEPS - k
-            return k - SWEEPS, k
-
-        for k in range(1, SWEEPS + 1):
-            a, b = span(k)
-            for x in range(a, b):
-                new = stencil(value(k - 1, x - 1), value(k - 1, x), value(k - 1, x + 1), start(1, x), start(2, x))
-                if k == SWEEPS:
-                    last[side, x - a] = new[:ny, :nz]
-                else:
-                    steps[k - 1][side, x - a] = new
-        a, b = span(SWEEPS)
-        copy = pltpu.make_async_copy(last.at[side], out.at[a:b], sem.at[1 + side])
+        a, b = span(side, SWEEPS)
+        copy = pltpu.make_async_copy(last.at[side], out.at[a:b], sem.at[side])
         copy.start()
         wait.append(copy)
     for copy in wait:
@@ -329,31 +341,39 @@
     nx, ny, nz = u.shape
     cells = nx * ny * nz
     raw = (u, r, s)
+    fixed = [pltpu.with_memory_space_constraint(v, pltpu.HBM) for v in raw]
     scratch = [pltpu.VMEM((3, 2, nx, 8, nz), F32), pltpu.SemaphoreType.DMA((3, 2))]
-    fixed = [pltpu.with_memory_space_constraint(v, pltpu.HBM) for v in raw]
-    sent = call(pack_y, [(3, nx // 2, 8, nz)] * 2, fixed, cells // 4, scratch, 8, from_hbm=True)
+    sent = call(pack_y, [(3, nx // 2, 8, nz)] * 2, fixed, cells // 4, scratch, 8, hbm_in=range(3))
     y = swap(sent, "gy")
     sent = call(pack_z, [(3, nx // 32, ny, 128)] * 2, raw, cells)
     z = swap(sent, "gz")
     sent = call(pack_x, [(len(LAYERS), ny, nz)] * 2, raw, cells // 8)
     x = swap(sent, "gx")
+    (w,) = call(weigh, [u.shape], (s,), 8 * cells)
     sent = call(pack_yz, [(3, nx // 32, 8, 128)] * 2, z, cells // 64)
     b = swap(sent, "gy")
-    *t, w = call(unpack_z, [(nx, ny, 128)] * 3 + [u.shape], (*z, s), 8 * cells)
-    rows = call(unpack_y, [(nx, 8, nz)] * 3 + [(nx, 8, 128)] * 3, (*y, *b), cells)
-    yy, e = rows[:3], rows[3:]
-    sent = call(pack_edges, [(len(LAYERS) + 3, 8, nz)] * 2, (*yy, *t, *e), cells // 8)
-    c = swap(sent, "gx")
+    t = call(unpack_z, [(nx, ny, 128)] * 3, z, 8 * cells)
+    yy = call(unpack_y, [(nx, 8, nz)] * 3, y, cells)
+    shape = (len(LAYERS) + 3, 8, nz)
+    *e, c_near, c_far = call(pack_edges, [(nx, 8, 128)] * 3 + [shape] * 2, (*b, *yy, *t), cells // 8)
+    c = swap((c_near, c_far), "gx")
     parts = [v for a, m in enumerate((u, r, w)) for v in (m, yy[a], t[a], e[a])]
     block = (ny + 2 * WIDE, nz + 128)
-    scratch = [pltpu.VMEM((nx,) + block, F32)] * 3
-    body, *ends = call(centre, [u.shape] + [(4,) + block] * 3, parts, 60 * cells, scratch, 16)
+    _, _, first, stop = steps_of(nx)
+    scratch = [pltpu.VMEM(u.shape, F32), pltpu.SemaphoreType.DMA] + [pltpu.VMEM((nx,) + block, F32)] * 3
+    left = (nx - WIDE - stop + first - WIDE, ny, nz)
+    out, rest, *ends = call(
+        centre, [u.shape, left] + [(4,) + block] * 3, parts, 60 * cells, scratch, 16, hbm_out=(0,)
+    )
     scratch = [
         pltpu.VMEM((2, len(LAYERS)) + block, F32),
         pltpu.VMEM((2, WIDE, ny, nz), F32),
-        pltpu.SemaphoreType.DMA((3,)),
+        pltpu.SemaphoreType.DMA((4,)),
     ] + [pltpu.VMEM((2, SWEEPS) + block, F32)] * 3
-    (out,) = call(tail, [u.shape], (*parts, body, *ends, *x, *c), 8 * cells, scratch, 8, to_hbm=True)
+    operands = (*parts, out, rest, *ends, *x, *c)
+    (out,) = call(
+        tail, [u.shape], operands, 8 * cells, scratch, 8, hbm_in=(12,), hbm_out=(0,), aliases={12: 0}
+    )
     return out
 
 

time: 42.7 us -> 41.8 us (0.979)
  waiting for transfers between devices: 5.48 us -> 4.83 us
    ppermute x10, waiting for transfers between devices: 5.48 us -> 4.83 us  [swap(): return (lax.ppermute(sent[0], axis, near), lax.ppermute(sent[1], axis, far))]
    pallas_call x9 -> x10, Pallas kernels: 18.2 us -> 18.1 us  [call(): pl.pallas_call(kernel, out_shape=[jax.ShapeDtypeStruct(s, F32) for s in o...]
  transfers between devices with their start and end apart: 10 -> 10, of which waited for: 3 -> 2; matrix products, arithmetic and copies ran while one was open for 0% -> 0% of each run, Pallas kernels for 33% -> 34%
where the time goes in v1:
time: 41.8 us; the launch traced here: 41.3 us
  starting transfers between devices  18.2 us (44%)
  Pallas kernels  18.1 us (43%)
  waiting for transfers between devices  4.83 us (12%)
    ppermute x10, starting transfers between devices, swap(): return (lax.ppermute(sent[0], axis, near), lax.ppermute(sent[1], axis, far))  18.2 us
    pallas_call x10, Pallas kernels, call(): pl.pallas_call(kernel, out_shape=[jax.ShapeDtypeStruct(s, F32) for s in o...  18.1 us
    ppermute x10, waiting for transfers between devices, swap(): return (lax.ppermute(sent[0], axis, near), lax.ppermute(sent[1], axis, far))  4.83 us
  transfers between devices with their start and end apart: 10, of which 2 were waited for; matrix products, arithmetic and copies ran while one was open for 0% of the time, Pallas kernels for 34%

profile of v1, /device:TPU:1, one launch (start us, length us, event | category | flops | bytes accessed | tf_op | source)
XLA Modules:
  0.0 41.3 jit_solution(3547183120925217722)
XLA Ops:
  0.0 0.0 copy-start.1
  0.0 0.0 copy-start
  0.0 0.0 copy-start.2
  0.0 2.1 %shard_map.37 = (f32[3,32,8,256]{3,2,1,0:T(8,128)S(1)}, f32[3,32,8,256]{3,2,1,0:T(8,128)S(1)}) custom-call(f32[64,32,256]{2,1,0:T(8,128)} %refs_0_.3, f32[64,32,256]{2,1,0:T(8,128)} %refs_4_.3, f32[64,32,256]{2,1,0:T(8,128)} %s.7), custom_call_target="tpu_custom_call" | custom-call | flops 131072 | bytes 1048576 | tf_op jit(solution)/shard_map/pallas_call | solution.py:19
  2.1 3.3 %collective-permute-start = (f32[3,32,8,256]{3,2,1,0:T(8,128)S(1)}, f32[3,32,8,256]{3,2,1,0:T(8,128)S(1)}, u32[]{:S(2)}, u32[]{:S(2)}) collective-permute-start(f32[3,32,8,256]{3,2,1,0:T(8,128)S(1)} %get-tuple-element.29), channel_id=1, source_target_pairs={{0,4},{4,0},{8,12},{12,8},{16,20},{20,16},{24,28},{28,24},{32,36},... | collective-permute-start | bytes 2359304 | tf_op jit(solution)/shard_map/ppermute | solution.py:39
  5.4 0.0 collective-permute-start.1
  5.4 0.0 copy-done.1
  5.4 0.0 copy-done
  5.4 0.0 copy-done.2
  5.5 1.2 %shard_map.39 = (f32[3,2,32,128]{3,2,1,0:T(8,128)S(1)}, f32[3,2,32,128]{3,2,1,0:T(8,128)S(1)}) custom-call(f32[64,32,256]{2,1,0:T(8,128)S(1)} %copy-done, f32[64,32,256]{2,1,0:T(8,128)S(1)} %copy-done.1, f32[64,32,256]{2,1,0:T(8,128)S(1)} %copy-done.2), custom_call_target="tpu_custom_call" | custom-call | flops 524288 | bytes 1048576 | tf_op jit(solution)/shard_map/pallas_call | solution.py:19
  6.7 1.2 %collective-permute-start.2 = (f32[3,2,32,128]{3,2,1,0:T(8,128)S(1)}, f32[3,2,32,128]{3,2,1,0:T(8,128)S(1)}, u32[]{:S(2)}, u32[]{:S(2)}) collective-permute-start(f32[3,2,32,128]{3,2,1,0:T(8,128)S(1)} %get-tuple-element.32), channel_id=1, source_target_pairs={{0,1},{1,0},{2,3},{3,2},{4,5},{5,4},{6,7},{7,6},{8,9},{9,8},{10,11... | collective-permute-start | bytes 294920 | tf_op jit(solution)/shard_map/ppermute | solution.py:39
  8.0 1.4 %collective-permute-start.6 = (f32[10,32,256]{2,1,0:T(8,128)S(1)}, f32[10,32,256]{2,1,0:T(8,128)S(1)}, u32[]{:S(2)}, u32[]{:S(2)}) collective-permute-start(f32[10,32,256]{2,1,0:T(8,128)S(1)} %get-tuple-element.49), channel_id=1, source_target_pairs={{0,64},{64,0},{128,192},{192,128},{1,65},{65,1},{129,193},{193,129... | collective-permute-start | bytes 983048 | tf_op jit(solution)/shard_map/ppermute | solution.py:39
  9.3 1.9 %collective-permute-start.7 = (f32[10,32,256]{2,1,0:T(8,128)S(1)}, f32[10,32,256]{2,1,0:T(8,128)S(1)}, u32[]{:S(2)}, u32[]{:S(2)}) collective-permute-start(f32[10,32,256]{2,1,0:T(8,128)S(1)} %get-tuple-element.50), channel_id=1, source_target_pairs={{0,192},{64,128},{128,64},{192,0},{1,193},{65,129},{129,65},{193,1... | collective-permute-start | bytes 983048 | tf_op jit(solution)/shard_map/ppermute | solution.py:39
  11.2 0.0 collective-permute-done.2.za
  11.2 1.8 %collective-permute-start.3 = (f32[3,2,32,128]{3,2,1,0:T(8,128)S(1)}, f32[3,2,32,128]{3,2,1,0:T(8,128)S(1)}, u32[]{:S(2)}, u32[]{:S(2)}) collective-permute-start(f32[3,2,32,128]{3,2,1,0:T(8,128)S(1)} %get-tuple-element.33), channel_id=1, source_target_pairs={{0,3},{1,2},{2,1},{3,0},{4,7},{5,6},{6,5},{7,4},{8,11},{9,10},{10,... | collective-permute-start | bytes 294920 | tf_op jit(solution)/shard_map/ppermute | solution.py:39
  13.1 3.2 %collective-permute-done.3.zb = f32[3,2,32,128]{3,2,1,0:T(8,128)S(1)} collective-permute-done((f32[3,2,32,128]{3,2,1,0:T(8,128)S(1)}, f32[3,2,32,128]{3,2,1,0:T(8,128)S(1)}, u32[]{:S(2)}, u32[]{:S(2)}) %collective-permute-start.3) | collective-permute-done | bytes 98336 | tf_op jit(solution)/shard_map/ppermute | solution.py:39
  16.2 6.1 %collective-permute-start.4 = (f32[3,2,8,128]{3,2,1,0:T(8,128)S(1)}, f32[3,2,8,128]{3,2,1,0:T(8,128)S(1)}, u32[]{:S(2)}, u32[]{:S(2)}) collective-permute-start(f32[3,2,8,128]{3,2,1,0:T(8,128)S(1)} %get-tuple-element.35), channel_id=1, source_target_pairs={{0,4},{4,0},{8,12},{12,8},{16,20},{20,16},{24,28},{28,24},{32,36},... | collective-permute-start | bytes 73736 | tf_op jit(solution)/shard_map/ppermute | solution.py:39
  22.4 0.0 collective-permute-done.near
  22.4 0.0 collective-permute-start.5
  22.4 1.2 %shard_map.40 = (f32[64,32,128]{2,1,0:T(8,128)S(1)}, f32[64,32,128]{2,1,0:T(8,128)S(1)}, f32[64,32,128]{2,1,0:T(8,128)S(1)}) custom-call(f32[3,2,32,128]{3,2,1,0:T(8,128)S(1)} %collective-permute-done.2.za, f32[3,2,32,128]{3,2,1,0:T(8,128)S(1)} %collective-permute-done.3.zb), custom_call_target="tpu_custom_call" | custom-call | flops 4194304 | bytes 1048576 | tf_op jit(solution)/shard_map/pallas_call | solution.py:19
  23.6 0.0 collective-permute-done.1.far
  23.6 0.3 shard_map.38
  24.0 0.0 collective-permute-done.4.b_near
  24.0 1.7 %collective-permute-done.5.b_far = f32[3,2,8,128]{3,2,1,0:T(8,128)S(1)} collective-permute-done((f32[3,2,8,128]{3,2,1,0:T(8,128)S(1)}, f32[3,2,8,128]{3,2,1,0:T(8,128)S(1)}, u32[]{:S(2)}, u32[]{:S(2)}) %collective-permute-start.5) | collective-permute-done | bytes 24608 | tf_op jit(solution)/shard_map/ppermute | solution.py:39
  25.6 0.4 %shard_map.42 = (f32[64,8,128]{2,1,0:T(8,128)S(1)}, f32[64,8,128]{2,1,0:T(8,128)S(1)}, f32[64,8,128]{2,1,0:T(8,128)S(1)}, f32[13,8,256]{2,1,0:T(8,128)S(1)}, f32[13,8,256]{2,1,0:T(8,128)S(1)}) custom-call(f32[3,2,8,128]{3,2,1,0:T(8,128)S(1)} %collective-permute-done.4.b_near, f32[3,2,8,128]{3,2,1,0:T(8,128)S(1)} %collective-permute-done.5.b_far, ...), custom_call_target="tpu_custom_call" | custom-call | flops 65536 | bytes 1048576 | tf_op jit(solution)/shard_map/pallas_call | solution.py:19
  26.0 0.6 %collective-permute-start.8 = (f32[13,8,256]{2,1,0:T(8,128)S(1)}, f32[13,8,256]{2,1,0:T(8,128)S(1)}, u32[]{:S(2)}, u32[]{:S(2)}) collective-permute-start(f32[13,8,256]{2,1,0:T(8,128)S(1)} %get-tuple-element.51), channel_id=1, source_target_pairs={{0,64},{64,0},{128,192},{192,128},{1,65},{65,1},{129,193},{193,129... | collective-permute-start | bytes 319496 | tf_op jit(solution)/shard_map/ppermute | solution.py:39
  26.7 1.9 %collective-permute-start.9 = (f32[13,8,256]{2,1,0:T(8,128)S(1)}, f32[13,8,256]{2,1,0:T(8,128)S(1)}, u32[]{:S(2)}, u32[]{:S(2)}) collective-permute-start(f32[13,8,256]{2,1,0:T(8,128)S(1)} %get-tuple-element.52), channel_id=1, source_target_pairs={{0,192},{64,128},{128,64},{192,0},{1,193},{65,129},{129,65},{193,1... | collective-permute-start | bytes 319496 | tf_op jit(solution)/shard_map/ppermute | solution.py:39
  28.6 0.6 %shard_map.43.refs_8_ = f32[64,32,256]{2,1,0:T(8,128)S(1)} custom-call(f32[64,32,256]{2,1,0:T(8,128)S(1)} %copy-done.2), custom_call_target="tpu_custom_call" | custom-call | flops 4194304 | bytes 1048576 | tf_op jit(solution)/shard_map/pallas_call | solution.py:19
  29.1 10.2 %shard_map.44 = (f32[64,32,256]{2,1,0:T(8,128)}, f32[6,32,256]{2,1,0:T(8,128)S(1)}, f32[4,40,384]{2,1,0:T(8,128)S(1)}, f32[4,40,384]{2,1,0:T(8,128)S(1)}, f32[4,40,384]{2,1,0:T(8,128)S(1)}) custom-call(f32[64,32,256]{2,1,0:T(8,128)S(1)} %copy-done, f32[64,8,256]{2,1,0:T(8,128)S(1)} %get-tuple-element.31.yu.refs_1_, ...), custom_call_target="tpu_custom_call" | custom-call | flops 31457280 | bytes 1048576 | tf_op jit(solution)/shard_map/pallas_call | solution.py:19
  39.3 0.0 collective-permute-done.6.refs_17_
  39.3 0.0 collective-permute-done.7.refs_18_
  39.3 0.0 collective-permute-done.8.refs_19_
  39.3 0.0 collective-permute-done.9.refs_20_
  39.4 1.9 %shard_map.46 = f32[64,32,256]{2,1,0:T(8,128)} custom-call(f32[64,32,256]{2,1,0:T(8,128)S(1)} %copy-done, f32[64,8,256]{2,1,0:T(8,128)S(1)} %get-tuple-element.31.yu.refs_1_, f32[64,32,128]{2,1,0:T(8,128)S(1)} %get-tuple-element.34.tu.refs_2_, f32[64,8,128]{2,1,0:T(8,128)S(1)} %get-tuple-element.41.refs_3_, ...), custom_call_target="tpu_custom_call", output_to_operand_aliasing={{}: (12, {})} | custom-call | flops 4194304 | bytes 1048576 | tf_op jit(solution)/shard_map/pallas_call | solution.py:19
  (2 shorter events, 0.1 us)
Async XLA Ops:
  0.0 5.4 %copy-start.1 = (f32[64,32,256]{2,1,0:T(8,128)S(1)}, f32[64,32,256]{2,1,0:T(8,128)}, u32[]{:S(2)}) copy-start(f32[64,32,256]{2,1,0:T(8,128)} %refs_4_.3) | copy-start | bytes 6291460
  0.0 5.4 %copy-start = (f32[64,32,256]{2,1,0:T(8,128)S(1)}, f32[64,32,256]{2,1,0:T(8,128)}, u32[]{:S(2)}) copy-start(f32[64,32,256]{2,1,0:T(8,128)} %refs_0_.3) | copy-start | bytes 6291460
  0.0 5.4 %copy-start.2 = (f32[64,32,256]{2,1,0:T(8,128)S(1)}, f32[64,32,256]{2,1,0:T(8,128)}, u32[]{:S(2)}) copy-start(f32[64,32,256]{2,1,0:T(8,128)} %s.7) | copy-start | bytes 6291460
  2.1 20.2 %collective-permute-start = (f32[3,32,8,256]{3,2,1,0:T(8,128)S(1)}, f32[3,32,8,256]{3,2,1,0:T(8,128)S(1)}, u32[]{:S(2)}, u32[]{:S(2)}) collective-permute-start(f32[3,32,8,256]{3,2,1,0:T(8,128)S(1)} %get-tuple-element.29), channel_id=1, source_target_pairs={{0,4},{4,0},{8,12},{12,8},{16,20},{20,16},{24,28},{28,24},{32,36},... | collective-permute-start | bytes 2359304 | tf_op jit(solution)/shard_map/ppermute | solution.py:39
  5.4 18.2 %collective-permute-start.1 = (f32[3,32,8,256]{3,2,1,0:T(8,128)S(1)}, f32[3,32,8,256]{3,2,1,0:T(8,128)S(1)}, u32[]{:S(2)}, u32[]{:S(2)}) collective-permute-start(f32[3,32,8,256]{3,2,1,0:T(8,128)S(1)} %get-tuple-element.30), channel_id=1, source_target_pairs={{0,60},{4,8},{8,4},{12,16},{16,12},{20,24},{24,20},{28,32},{32,28}... | collective-permute-start | bytes 2359304 | tf_op jit(solution)/shard_map/ppermute | solution.py:39
  6.7 4.5 %collective-permute-start.2 = (f32[3,2,32,128]{3,2,1,0:T(8,128)S(1)}, f32[3,2,32,128]{3,2,1,0:T(8,128)S(1)}, u32[]{:S(2)}, u32[]{:S(2)}) collective-permute-start(f32[3,2,32,128]{3,2,1,0:T(8,128)S(1)} %get-tuple-element.32), channel_id=1, source_target_pairs={{0,1},{1,0},{2,3},{3,2},{4,5},{5,4},{6,7},{7,6},{8,9},{9,8},{10,11... | collective-permute-start | bytes 294920 | tf_op jit(solution)/shard_map/ppermute | solution.py:39
  8.0 31.4 %collective-permute-start.6 = (f32[10,32,256]{2,1,0:T(8,128)S(1)}, f32[10,32,256]{2,1,0:T(8,128)S(1)}, u32[]{:S(2)}, u32[]{:S(2)}) collective-permute-start(f32[10,32,256]{2,1,0:T(8,128)S(1)} %get-tuple-element.49), channel_id=1, source_target_pairs={{0,64},{64,0},{128,192},{192,128},{1,65},{65,1},{129,193},{193,129... | collective-permute-start | bytes 983048 | tf_op jit(solution)/shard_map/ppermute | solution.py:39
  9.3 30.0 %collective-permute-start.7 = (f32[10,32,256]{2,1,0:T(8,128)S(1)}, f32[10,32,256]{2,1,0:T(8,128)S(1)}, u32[]{:S(2)}, u32[]{:S(2)}) collective-permute-start(f32[10,32,256]{2,1,0:T(8,128)S(1)} %get-tuple-element.50), channel_id=1, source_target_pairs={{0,192},{64,128},{128,64},{192,0},{1,193},{65,129},{129,65},{193,1... | collective-permute-start | bytes 983048 | tf_op jit(solution)/shard_map/ppermute | solution.py:39
  11.2 5.0 %collective-permute-start.3 = (f32[3,2,32,128]{3,2,1,0:T(8,128)S(1)}, f32[3,2,32,128]{3,2,1,0:T(8,128)S(1)}, u32[]{:S(2)}, u32[]{:S(2)}) collective-permute-start(f32[3,2,32,128]{3,2,1,0:T(8,128)S(1)} %get-tuple-element.33), channel_id=1, source_target_pairs={{0,3},{1,2},{2,1},{3,0},{4,7},{5,6},{6,5},{7,4},{8,11},{9,10},{10,... | collective-permute-start | bytes 294920 | tf_op jit(solution)/shard_map/ppermute | solution.py:39
  16.2 7.7 %collective-permute-start.4 = (f32[3,2,8,128]{3,2,1,0:T(8,128)S(1)}, f32[3,2,8,128]{3,2,1,0:T(8,128)S(1)}, u32[]{:S(2)}, u32[]{:S(2)}) collective-permute-start(f32[3,2,8,128]{3,2,1,0:T(8,128)S(1)} %get-tuple-element.35), channel_id=1, source_target_pairs={{0,4},{4,0},{8,12},{12,8},{16,20},{20,16},{24,28},{28,24},{32,36},... | collective-permute-start | bytes 73736 | tf_op jit(solution)/shard_map/ppermute | solution.py:39
  22.4 3.3 %collective-permute-start.5 = (f32[3,2,8,128]{3,2,1,0:T(8,128)S(1)}, f32[3,2,8,128]{3,2,1,0:T(8,128)S(1)}, u32[]{:S(2)}, u32[]{:S(2)}) collective-permute-start(f32[3,2,8,128]{3,2,1,0:T(8,128)S(1)} %get-tuple-element.36), channel_id=1, source_target_pairs={{0,60},{4,8},{8,4},{12,16},{16,12},{20,24},{24,20},{28,32},{32,28}... | collective-permute-start | bytes 73736 | tf_op jit(solution)/shard_map/ppermute | solution.py:39
  26.0 13.3 %collective-permute-start.8 = (f32[13,8,256]{2,1,0:T(8,128)S(1)}, f32[13,8,256]{2,1,0:T(8,128)S(1)}, u32[]{:S(2)}, u32[]{:S(2)}) collective-permute-start(f32[13,8,256]{2,1,0:T(8,128)S(1)} %get-tuple-element.51), channel_id=1, source_target_pairs={{0,64},{64,0},{128,192},{192,128},{1,65},{65,1},{129,193},{193,129... | collective-permute-start | bytes 319496 | tf_op jit(solution)/shard_map/ppermute | solution.py:39
  26.7 12.7 %collective-permute-start.9 = (f32[13,8,256]{2,1,0:T(8,128)S(1)}, f32[13,8,256]{2,1,0:T(8,128)S(1)}, u32[]{:S(2)}, u32[]{:S(2)}) collective-permute-start(f32[13,8,256]{2,1,0:T(8,128)S(1)} %get-tuple-element.52), channel_id=1, source_target_pairs={{0,192},{64,128},{128,64},{192,0},{1,193},{65,129},{129,65},{193,1... | collective-permute-start | bytes 319496 | tf_op jit(solution)/shard_map/ppermute | solution.py:39

commit v2 on v1

--- a/solution.py
+++ b/solution.py
@@ -207,7 +207,7 @@
     return jnp.concatenate([left, jnp.concatenate([t[x], e[x]], 0)], 1)
 
 
-PLANES = 2
+PLANES = 4
 
 
 def planes(i):
@@ -240,8 +240,11 @@
     def one(k, x):
         r, w = whole(x, *r0), whole(x, *w0)
         new = stencil(plane(k, x - 1), plane(k, x), plane(k, x + 1), r, w)
-        if k < SWEEPS - 1:
+        if k < SWEEPS - 2:
             steps[k][x] = new
+        elif k == SWEEPS - 2:
+            steps[k][x, :, :nz] = new[:, :nz]
+            steps[k][x, :ny, nz:] = new[:ny, nz:]
         elif isinstance(x, int):
             rest[x - stop if x >= stop else nx - WIDE - stop + x - WIDE] = new[:ny, :nz]
         else:
@@ -324,10 +327,16 @@
                 x = span(side, k)[0] + j
                 near = [value(side, k - 1, x + d) for d in (-1, 0, 1)]
                 new = stencil(*near, start(1, x), start(2, x))
+                reach = SWEEPS - k - max(0, x - nx + 1, -x)
                 if k == SWEEPS:
                     last[side, j] = new[:ny, :nz]
+                elif reach > 1:
+                    steps[k - 1][side, j] = new
                 else:
-                    steps[k - 1][side, j] = new
+                    steps[k - 1][side, j, :ny, :nz] = new[:ny, :nz]
+                    if reach == 1:
+                        steps[k - 1][side, j, ny:, :nz] = new[ny:, :nz]
+                        steps[k - 1][side, j, :ny, nz:] = new[:ny, nz:]
     for side in (0, 1):
         a, b = span(side, SWEEPS)
         copy = pltpu.make_async_copy(last.at[side], out.at[a:b], sem.at[side])

time: 41.8 us -> 40.1 us (0.959)
  Pallas kernels: 18.1 us -> 16.5 us
    pallas_call x10, Pallas kernels: 18.1 us -> 16.5 us  [call(): pl.pallas_call(kernel, out_shape=[jax.ShapeDtypeStruct(s, F32) for s in o...]
  transfers between devices with their start and end apart: 10 -> 10, of which waited for: 2 -> 2; matrix products, arithmetic and copies ran while one was open for 0% -> 0% of each run, Pallas kernels for 34% -> 31%
where the time goes in v2:
time: 40.1 us; the launch traced here: 39.7 us
  starting transfers between devices  18.2 us (45%)
  Pallas kernels  16.5 us (41%)
  waiting for transfers between devices  4.83 us (12%)
    ppermute x10, starting transfers between devices, swap(): return (lax.ppermute(sent[0], axis, near), lax.ppermute(sent[1], axis, far))  18.2 us
    pallas_call x10, Pallas kernels, call(): pl.pallas_call(kernel, out_shape=[jax.ShapeDtypeStruct(s, F32) for s in o...  16.5 us
    ppermute x10, waiting for transfers between devices, swap(): return (lax.ppermute(sent[0], axis, near), lax.ppermute(sent[1], axis, far))  4.83 us
  transfers between devices with their start and end apart: 10, of which 2 were waited for; matrix products, arithmetic and copies ran while one was open for 0% of the time, Pallas kernels for 31%

profile of v2, /device:TPU:1, one launch (start us, length us, event | category | flops | bytes accessed | tf_op | source)
XLA Modules:
  0.0 39.7 jit_solution(294240125773580713)
XLA Ops:
  0.0 0.0 copy-start.1
  0.0 0.0 copy-start
  0.0 0.0 copy-start.2
  0.0 2.1 %shard_map.37 = (f32[3,32,8,256]{3,2,1,0:T(8,128)S(1)}, f32[3,32,8,256]{3,2,1,0:T(8,128)S(1)}) custom-call(f32[64,32,256]{2,1,0:T(8,128)} %refs_0_.3, f32[64,32,256]{2,1,0:T(8,128)} %refs_4_.3, f32[64,32,256]{2,1,0:T(8,128)} %s.7), custom_call_target="tpu_custom_call" | custom-call | flops 131072 | bytes 1048576 | tf_op jit(solution)/shard_map/pallas_call | solution.py:19
  2.1 3.3 %collective-permute-start = (f32[3,32,8,256]{3,2,1,0:T(8,128)S(1)}, f32[3,32,8,256]{3,2,1,0:T(8,128)S(1)}, u32[]{:S(2)}, u32[]{:S(2)}) collective-permute-start(f32[3,32,8,256]{3,2,1,0:T(8,128)S(1)} %get-tuple-element.29), channel_id=1, source_target_pairs={{0,4},{4,0},{8,12},{12,8},{16,20},{20,16},{24,28},{28,24},{32,36},... | collective-permute-start | bytes 2359304 | tf_op jit(solution)/shard_map/ppermute | solution.py:39
  5.4 0.0 collective-permute-start.1
  5.4 0.0 copy-done.1
  5.4 0.0 copy-done
  5.4 0.0 copy-done.2
  5.5 1.2 %shard_map.39 = (f32[3,2,32,128]{3,2,1,0:T(8,128)S(1)}, f32[3,2,32,128]{3,2,1,0:T(8,128)S(1)}) custom-call(f32[64,32,256]{2,1,0:T(8,128)S(1)} %copy-done, f32[64,32,256]{2,1,0:T(8,128)S(1)} %copy-done.1, f32[64,32,256]{2,1,0:T(8,128)S(1)} %copy-done.2), custom_call_target="tpu_custom_call" | custom-call | flops 524288 | bytes 1048576 | tf_op jit(solution)/shard_map/pallas_call | solution.py:19
  6.7 1.2 %collective-permute-start.2 = (f32[3,2,32,128]{3,2,1,0:T(8,128)S(1)}, f32[3,2,32,128]{3,2,1,0:T(8,128)S(1)}, u32[]{:S(2)}, u32[]{:S(2)}) collective-permute-start(f32[3,2,32,128]{3,2,1,0:T(8,128)S(1)} %get-tuple-element.32), channel_id=1, source_target_pairs={{0,1},{1,0},{2,3},{3,2},{4,5},{5,4},{6,7},{7,6},{8,9},{9,8},{10,11... | collective-permute-start | bytes 294920 | tf_op jit(solution)/shard_map/ppermute | solution.py:39
  8.0 1.4 %collective-permute-start.6 = (f32[10,32,256]{2,1,0:T(8,128)S(1)}, f32[10,32,256]{2,1,0:T(8,128)S(1)}, u32[]{:S(2)}, u32[]{:S(2)}) collective-permute-start(f32[10,32,256]{2,1,0:T(8,128)S(1)} %get-tuple-element.49), channel_id=1, source_target_pairs={{0,64},{64,0},{128,192},{192,128},{1,65},{65,1},{129,193},{193,129... | collective-permute-start | bytes 983048 | tf_op jit(solution)/shard_map/ppermute | solution.py:39
  9.3 1.9 %collective-permute-start.7 = (f32[10,32,256]{2,1,0:T(8,128)S(1)}, f32[10,32,256]{2,1,0:T(8,128)S(1)}, u32[]{:S(2)}, u32[]{:S(2)}) collective-permute-start(f32[10,32,256]{2,1,0:T(8,128)S(1)} %get-tuple-element.50), channel_id=1, source_target_pairs={{0,192},{64,128},{128,64},{192,0},{1,193},{65,129},{129,65},{193,1... | collective-permute-start | bytes 983048 | tf_op jit(solution)/shard_map/ppermute | solution.py:39
  11.2 0.0 collective-permute-done.2.za
  11.2 1.8 %collective-permute-start.3 = (f32[3,2,32,128]{3,2,1,0:T(8,128)S(1)}, f32[3,2,32,128]{3,2,1,0:T(8,128)S(1)}, u32[]{:S(2)}, u32[]{:S(2)}) collective-permute-start(f32[3,2,32,128]{3,2,1,0:T(8,128)S(1)} %get-tuple-element.33), channel_id=1, source_target_pairs={{0,3},{1,2},{2,1},{3,0},{4,7},{5,6},{6,5},{7,4},{8,11},{9,10},{10,... | collective-permute-start | bytes 294920 | tf_op jit(solution)/shard_map/ppermute | solution.py:39
  13.1 3.2 %collective-permute-done.3.zb = f32[3,2,32,128]{3,2,1,0:T(8,128)S(1)} collective-permute-done((f32[3,2,32,128]{3,2,1,0:T(8,128)S(1)}, f32[3,2,32,128]{3,2,1,0:T(8,128)S(1)}, u32[]{:S(2)}, u32[]{:S(2)}) %collective-permute-start.3) | collective-permute-done | bytes 98336 | tf_op jit(solution)/shard_map/ppermute | solution.py:39
  16.2 6.1 %collective-permute-start.4 = (f32[3,2,8,128]{3,2,1,0:T(8,128)S(1)}, f32[3,2,8,128]{3,2,1,0:T(8,128)S(1)}, u32[]{:S(2)}, u32[]{:S(2)}) collective-permute-start(f32[3,2,8,128]{3,2,1,0:T(8,128)S(1)} %get-tuple-element.35), channel_id=1, source_target_pairs={{0,4},{4,0},{8,12},{12,8},{16,20},{20,16},{24,28},{28,24},{32,36},... | collective-permute-start | bytes 73736 | tf_op jit(solution)/shard_map/ppermute | solution.py:39
  22.4 0.0 collective-permute-done.near
  22.4 0.0 collective-permute-start.5
  22.4 1.2 %shard_map.40 = (f32[64,32,128]{2,1,0:T(8,128)S(1)}, f32[64,32,128]{2,1,0:T(8,128)S(1)}, f32[64,32,128]{2,1,0:T(8,128)S(1)}) custom-call(f32[3,2,32,128]{3,2,1,0:T(8,128)S(1)} %collective-permute-done.2.za, f32[3,2,32,128]{3,2,1,0:T(8,128)S(1)} %collective-permute-done.3.zb), custom_call_target="tpu_custom_call" | custom-call | flops 4194304 | bytes 1048576 | tf_op jit(solution)/shard_map/pallas_call | solution.py:19
  23.6 0.0 collective-permute-done.1.far
  23.6 0.3 shard_map.38
  24.0 0.0 collective-permute-done.4.b_near
  24.0 1.7 %collective-permute-done.5.b_far = f32[3,2,8,128]{3,2,1,0:T(8,128)S(1)} collective-permute-done((f32[3,2,8,128]{3,2,1,0:T(8,128)S(1)}, f32[3,2,8,128]{3,2,1,0:T(8,128)S(1)}, u32[]{:S(2)}, u32[]{:S(2)}) %collective-permute-start.5) | collective-permute-done | bytes 24608 | tf_op jit(solution)/shard_map/ppermute | solution.py:39
  25.6 0.4 %shard_map.42 = (f32[64,8,128]{2,1,0:T(8,128)S(1)}, f32[64,8,128]{2,1,0:T(8,128)S(1)}, f32[64,8,128]{2,1,0:T(8,128)S(1)}, f32[13,8,256]{2,1,0:T(8,128)S(1)}, f32[13,8,256]{2,1,0:T(8,128)S(1)}) custom-call(f32[3,2,8,128]{3,2,1,0:T(8,128)S(1)} %collective-permute-done.4.b_near, f32[3,2,8,128]{3,2,1,0:T(8,128)S(1)} %collective-permute-done.5.b_far, ...), custom_call_target="tpu_custom_call" | custom-call | flops 65536 | bytes 1048576 | tf_op jit(solution)/shard_map/pallas_call | solution.py:19
  26.0 0.6 %collective-permute-start.8 = (f32[13,8,256]{2,1,0:T(8,128)S(1)}, f32[13,8,256]{2,1,0:T(8,128)S(1)}, u32[]{:S(2)}, u32[]{:S(2)}) collective-permute-start(f32[13,8,256]{2,1,0:T(8,128)S(1)} %get-tuple-element.51), channel_id=1, source_target_pairs={{0,64},{64,0},{128,192},{192,128},{1,65},{65,1},{129,193},{193,129... | collective-permute-start | bytes 319496 | tf_op jit(solution)/shard_map/ppermute | solution.py:39
  26.7 1.9 %collective-permute-start.9 = (f32[13,8,256]{2,1,0:T(8,128)S(1)}, f32[13,8,256]{2,1,0:T(8,128)S(1)}, u32[]{:S(2)}, u32[]{:S(2)}) collective-permute-start(f32[13,8,256]{2,1,0:T(8,128)S(1)} %get-tuple-element.52), channel_id=1, source_target_pairs={{0,192},{64,128},{128,64},{192,0},{1,193},{65,129},{129,65},{193,1... | collective-permute-start | bytes 319496 | tf_op jit(solution)/shard_map/ppermute | solution.py:39
  28.6 0.6 %shard_map.43.refs_8_ = f32[64,32,256]{2,1,0:T(8,128)S(1)} custom-call(f32[64,32,256]{2,1,0:T(8,128)S(1)} %copy-done.2), custom_call_target="tpu_custom_call" | custom-call | flops 4194304 | bytes 1048576 | tf_op jit(solution)/shard_map/pallas_call | solution.py:19
  29.1 8.5 %shard_map.44 = (f32[64,32,256]{2,1,0:T(8,128)}, f32[16,32,256]{2,1,0:T(8,128)S(1)}, f32[4,40,384]{2,1,0:T(8,128)S(1)}, f32[4,40,384]{2,1,0:T(8,128)S(1)}, f32[4,40,384]{2,1,0:T(8,128)S(1)}) custom-call(f32[64,32,256]{2,1,0:T(8,128)S(1)} %copy-done, f32[64,8,256]{2,1,0:T(8,128)S(1)} %get-tuple-element.31.yu.refs_1_, ...), custom_call_target="tpu_custom_call" | custom-call | flops 31457280 | bytes 1048576 | tf_op jit(solution)/shard_map/pallas_call | solution.py:19
  37.6 0.0 collective-permute-done.6.refs_17_
  37.6 0.0 collective-permute-done.7.refs_18_
  37.7 0.0 collective-permute-done.8.refs_19_
  37.7 0.0 collective-permute-done.9.refs_20_
  37.7 2.0 %shard_map.46 = f32[64,32,256]{2,1,0:T(8,128)} custom-call(f32[64,32,256]{2,1,0:T(8,128)S(1)} %copy-done, f32[64,8,256]{2,1,0:T(8,128)S(1)} %get-tuple-element.31.yu.refs_1_, f32[64,32,128]{2,1,0:T(8,128)S(1)} %get-tuple-element.34.tu.refs_2_, f32[64,8,128]{2,1,0:T(8,128)S(1)} %get-tuple-element.41.refs_3_, ...), custom_call_target="tpu_custom_call", output_to_operand_aliasing={{}: (12, {})} | custom-call | flops 4194304 | bytes 1048576 | tf_op jit(solution)/shard_map/pallas_call | solution.py:19
  (2 shorter events, 0.1 us)
Async XLA Ops:
  0.0 5.4 %copy-start.1 = (f32[64,32,256]{2,1,0:T(8,128)S(1)}, f32[64,32,256]{2,1,0:T(8,128)}, u32[]{:S(2)}) copy-start(f32[64,32,256]{2,1,0:T(8,128)} %refs_4_.3) | copy-start | bytes 6291460
  0.0 5.4 %copy-start = (f32[64,32,256]{2,1,0:T(8,128)S(1)}, f32[64,32,256]{2,1,0:T(8,128)}, u32[]{:S(2)}) copy-start(f32[64,32,256]{2,1,0:T(8,128)} %refs_0_.3) | copy-start | bytes 6291460
  0.0 5.4 %copy-start.2 = (f32[64,32,256]{2,1,0:T(8,128)S(1)}, f32[64,32,256]{2,1,0:T(8,128)}, u32[]{:S(2)}) copy-start(f32[64,32,256]{2,1,0:T(8,128)} %s.7) | copy-start | bytes 6291460
  2.1 20.2 %collective-permute-start = (f32[3,32,8,256]{3,2,1,0:T(8,128)S(1)}, f32[3,32,8,256]{3,2,1,0:T(8,128)S(1)}, u32[]{:S(2)}, u32[]{:S(2)}) collective-permute-start(f32[3,32,8,256]{3,2,1,0:T(8,128)S(1)} %get-tuple-element.29), channel_id=1, source_target_pairs={{0,4},{4,0},{8,12},{12,8},{16,20},{20,16},{24,28},{28,24},{32,36},... | collective-permute-start | bytes 2359304 | tf_op jit(solution)/shard_map/ppermute | solution.py:39
  5.4 18.2 %collective-permute-start.1 = (f32[3,32,8,256]{3,2,1,0:T(8,128)S(1)}, f32[3,32,8,256]{3,2,1,0:T(8,128)S(1)}, u32[]{:S(2)}, u32[]{:S(2)}) collective-permute-start(f32[3,32,8,256]{3,2,1,0:T(8,128)S(1)} %get-tuple-element.30), channel_id=1, source_target_pairs={{0,60},{4,8},{8,4},{12,16},{16,12},{20,24},{24,20},{28,32},{32,28}... | collective-permute-start | bytes 2359304 | tf_op jit(solution)/shard_map/ppermute | solution.py:39
  6.7 4.5 %collective-permute-start.2 = (f32[3,2,32,128]{3,2,1,0:T(8,128)S(1)}, f32[3,2,32,128]{3,2,1,0:T(8,128)S(1)}, u32[]{:S(2)}, u32[]{:S(2)}) collective-permute-start(f32[3,2,32,128]{3,2,1,0:T(8,128)S(1)} %get-tuple-element.32), channel_id=1, source_target_pairs={{0,1},{1,0},{2,3},{3,2},{4,5},{5,4},{6,7},{7,6},{8,9},{9,8},{10,11... | collective-permute-start | bytes 294920 | tf_op jit(solution)/shard_map/ppermute | solution.py:39
  8.0 29.7 %collective-permute-start.6 = (f32[10,32,256]{2,1,0:T(8,128)S(1)}, f32[10,32,256]{2,1,0:T(8,128)S(1)}, u32[]{:S(2)}, u32[]{:S(2)}) collective-permute-start(f32[10,32,256]{2,1,0:T(8,128)S(1)} %get-tuple-element.49), channel_id=1, source_target_pairs={{0,64},{64,0},{128,192},{192,128},{1,65},{65,1},{129,193},{193,129... | collective-permute-start | bytes 983048 | tf_op jit(solution)/shard_map/ppermute | solution.py:39
  9.3 28.3 %collective-permute-start.7 = (f32[10,32,256]{2,1,0:T(8,128)S(1)}, f32[10,32,256]{2,1,0:T(8,128)S(1)}, u32[]{:S(2)}, u32[]{:S(2)}) collective-permute-start(f32[10,32,256]{2,1,0:T(8,128)S(1)} %get-tuple-element.50), channel_id=1, source_target_pairs={{0,192},{64,128},{128,64},{192,0},{1,193},{65,129},{129,65},{193,1... | collective-permute-start | bytes 983048 | tf_op jit(solution)/shard_map/ppermute | solution.py:39
  11.2 5.0 %collective-permute-start.3 = (f32[3,2,32,128]{3,2,1,0:T(8,128)S(1)}, f32[3,2,32,128]{3,2,1,0:T(8,128)S(1)}, u32[]{:S(2)}, u32[]{:S(2)}) collective-permute-start(f32[3,2,32,128]{3,2,1,0:T(8,128)S(1)} %get-tuple-element.33), channel_id=1, source_target_pairs={{0,3},{1,2},{2,1},{3,0},{4,7},{5,6},{6,5},{7,4},{8,11},{9,10},{10,... | collective-permute-start | bytes 294920 | tf_op jit(solution)/shard_map/ppermute | solution.py:39
  16.2 7.7 %collective-permute-start.4 = (f32[3,2,8,128]{3,2,1,0:T(8,128)S(1)}, f32[3,2,8,128]{3,2,1,0:T(8,128)S(1)}, u32[]{:S(2)}, u32[]{:S(2)}) collective-permute-start(f32[3,2,8,128]{3,2,1,0:T(8,128)S(1)} %get-tuple-element.35), channel_id=1, source_target_pairs={{0,4},{4,0},{8,12},{12,8},{16,20},{20,16},{24,28},{28,24},{32,36},... | collective-permute-start | bytes 73736 | tf_op jit(solution)/shard_map/ppermute | solution.py:39
  22.4 3.3 %collective-permute-start.5 = (f32[3,2,8,128]{3,2,1,0:T(8,128)S(1)}, f32[3,2,8,128]{3,2,1,0:T(8,128)S(1)}, u32[]{:S(2)}, u32[]{:S(2)}) collective-permute-start(f32[3,2,8,128]{3,2,1,0:T(8,128)S(1)} %get-tuple-element.36), channel_id=1, source_target_pairs={{0,60},{4,8},{8,4},{12,16},{16,12},{20,24},{24,20},{28,32},{32,28}... | collective-permute-start | bytes 73736 | tf_op jit(solution)/shard_map/ppermute | solution.py:39
  26.0 11.6 %collective-permute-start.8 = (f32[13,8,256]{2,1,0:T(8,128)S(1)}, f32[13,8,256]{2,1,0:T(8,128)S(1)}, u32[]{:S(2)}, u32[]{:S(2)}) collective-permute-start(f32[13,8,256]{2,1,0:T(8,128)S(1)} %get-tuple-element.51), channel_id=1, source_target_pairs={{0,64},{64,0},{128,192},{192,128},{1,65},{65,1},{129,193},{193,129... | collective-permute-start | bytes 319496 | tf_op jit(solution)/shard_map/ppermute | solution.py:39
  26.7 11.0 %collective-permute-start.9 = (f32[13,8,256]{2,1,0:T(8,128)S(1)}, f32[13,8,256]{2,1,0:T(8,128)S(1)}, u32[]{:S(2)}, u32[]{:S(2)}) collective-permute-start(f32[13,8,256]{2,1,0:T(8,128)S(1)} %get-tuple-element.52), channel_id=1, source_target_pairs={{0,192},{64,128},{128,64},{192,0},{1,193},{65,129},{129,65},{193,1... | collective-permute-start | bytes 319496 | tf_op jit(solution)/shard_map/ppermute | solution.py:39

commit v3 on v2

--- a/solution.py
+++ b/solution.py
@@ -12,6 +12,7 @@
 VMEM = pl.BlockSpec(memory_space=pltpu.VMEM)
 HBM = pl.BlockSpec(memory_space=pltpu.HBM)
 F32 = jnp.float32
+CHUNK = 16
 LAYERS = [(a, k) for a, n in enumerate((WIDE, WIDE - 1, WIDE - 1)) for k in range(n)]
 
 
@@ -54,61 +55,42 @@
     return jnp.where(head, above, below), pltpu.roll(jnp.where(head, below, above), 4, 0)
 
 
-def pack_y(u, r, s, near, far, ends, sem):
-    ny = u.shape[1]
-    is_odd = odd("gy") == 1
-    copies = []
-    for a, ref in enumerate((u, r, s)):
-        for e, row in enumerate((0, ny - 8)):
-            copy = pltpu.make_async_copy(ref.at[:, row : row + 8, :], ends.at[a, e], sem.at[a, e])
-            copy.start()
-            copies.append(copy)
-    for a in range(3):
-        copies[2 * a].wait()
-        copies[2 * a + 1].wait()
-        for face, low in ((near, is_odd), (far, jnp.logical_not(is_odd))):
-            end = jnp.where(low, 0, 1)
-
-            def body(i, c, face=face, low=low, end=end, a=a):
-                face[a, i] = fold(ends[a, end, 2 * i], ends[a, end, 2 * i + 1], low)
-                return c
-
-            lax.fori_loop(0, u.shape[0] // 2, body, 0, unroll=8)
-
-
-def pack_x(u, r, s, near, far):
-    nx = u.shape[0]
-    is_odd = odd("gx") == 1
-    for face, low in ((near, is_odd), (far, jnp.logical_not(is_odd))):
-        put = 0
-        for ref, layers in ((u, WIDE), (r, WIDE - 1), (s, WIDE - 1)):
-            start = jnp.where(low, 0, nx - layers)
-            for k in range(layers):
-                face[put] = ref[start + k]
-                put += 1
-
-
-def pack_z(u, r, s, near, far):
+def pack(u, r, s, u_v, r_v, s_v, y_near, y_far, z_near, z_far, x_near, x_far, sem):
     nx, ny, nz = u.shape
+    y_odd, z_odd, x_odd = odd("gy") == 1, odd("gz") == 1, odd("gx") == 1
+    held = (u_v, r_v, s_v)
+    copies = {}
+    for c in range(nx // CHUNK):
+        at = pl.ds(c * CHUNK, CHUNK)
+        for a, ref in enumerate((u, r, s)):
+            copies[c, a] = pltpu.make_async_copy(ref.at[at], held[a].at[at], sem.at[c, a])
+            copies[c, a].start()
     block = iota((ny, 128), 1) // 4
     half = iota((ny, 128), 1) < 64
-    is_odd = odd("gz") == 1
-    for a, ref in enumerate((u, r, s)):
-
-        def body(g, c, ref=ref, a=a):
-            low = jnp.zeros((ny, 128), F32)
-            high = low
-            for j in range(32):
-                x = g * 32 + j
+    for c in range(nx // CHUNK):
+        for a, ref in enumerate(held):
+            copies[c, a].wait()
+            for face, low in ((y_near, y_odd), (y_far, jnp.logical_not(y_odd))):
+                rows = pl.ds(pl.multiple_of(jnp.where(low, 0, ny - 8), 8), 8)
+                for i in range(c * CHUNK // 2, (c + 1) * CHUNK // 2):
+                    face[a, i] = fold(ref[2 * i, rows, :], ref[2 * i + 1, rows, :], low)
+            g = c * CHUNK // 32
+            first = c * CHUNK % 32 == 0
+            low = jnp.zeros((ny, 128), F32) if first else z_near[a, g]
+            high = jnp.zeros((ny, 128), F32) if first else z_far[a, g]
+            low, high = jnp.where(z_odd, low, high), jnp.where(z_odd, high, low)
+            for x in range(c * CHUNK, (c + 1) * CHUNK):
+                j = x % 32
                 both = jnp.where(half, ref[x, :, 0:128], ref[x, :, nz - 128 : nz])
                 both = pltpu.roll(both, 4 * j, 1) if j else both
                 low = jnp.where(block == j, both, low)
                 high = jnp.where(block == (j - 1) % 32, both, high)
-            near[a, g] = jnp.where(is_odd, low, high)
-            far[a, g] = jnp.where(is_odd, high, low)
-            return c
-
-        lax.fori_loop(0, nx // 32, body, 0)
+            z_near[a, g] = jnp.where(z_odd, low, high)
+            z_far[a, g] = jnp.where(z_odd, high, low)
+    for face, low in ((x_near, x_odd), (x_far, jnp.logical_not(x_odd))):
+        for q, (a, k) in enumerate(LAYERS):
+            layers = WIDE if a == 0 else WIDE - 1
+            face[q] = held[a][jnp.where(low, k, nx - layers + k)]
 
 
 def pack_yz(za, zb, near, far):
@@ -130,12 +112,69 @@
     return pltpu.roll(tile, 128 - 4 * j, 1) if j else tile
 
 
-def weigh(s, w):
+def begin(u, r, s, w, part, edge):
+    nx, ny, nz = u.shape
+    row, lane = iota((ny, nz), 0), iota((ny, nz), 1)
+    half = iota((ny, 128), 1) < 64
+    w[0] = weight(s[0])
+    w[nx - 1] = weight(s[nx - 1])
+
     def body(i, c):
-        w[i] = weight(s[i])
+        for x in (1 + 2 * i, 2 + 2 * i):
+            here = u[x]
+            beside = u[x - 1] + u[x + 1]
+            beside = beside + jnp.where(row == 0, 0.0, pltpu.roll(here, 1, 0))
+            beside = beside + jnp.where(row == ny - 1, 0.0, pltpu.roll(here, ny - 1, 0))
+            left, right = pltpu.roll(here, 1, 1), pltpu.roll(here, nz - 1, 1)
+            edge[x] = jnp.where(half, left[:, :128], right[:, nz - 128 :])
+            beside = beside + (jnp.where(lane == 0, 0.0, left) + jnp.where(lane == nz - 1, 0.0, right))
+            here_w = weight(s[x])
+            w[x] = here_w
+            part[x] = 0.2 * here + here_w * (r[x] + beside)
         return c
 
-    lax.fori_loop(0, s.shape[0], body, 0, unroll=2)
+    lax.fori_loop(0, (nx - 2) // 2, body, 0)
+
+
+def finish(x, u0, r0, w0, part, edge, new):
+    (u, yu, tu, eu), (_, yr, tr, er), (w, yw, tw, ew) = u0, r0, w0
+    ny, nz = u.shape[1:]
+    row, lane, lane_z = iota((8, nz), 0), iota((ny, 128), 1), iota((8, nz), 1)
+    lane_e = iota((8, 128), 1)
+    y, t, e = yu[x], tu[x], eu[x]
+    t_left, t_right = pltpu.roll(t, 1, 1), pltpu.roll(t, 127, 1)
+    e_left, e_right = pltpu.roll(e, 1, 1), pltpu.roll(e, 127, 1)
+    y_left, y_right = pltpu.roll(y, 1, 1), pltpu.roll(y, nz - 1, 1)
+    y_down, y_up = pltpu.roll(y, 1, 0), pltpu.roll(y, 7, 0)
+    halo = jnp.concatenate([jnp.where(lane == 0, t_left, 0.0), jnp.where(lane == 127, t_right, 0.0)], 1)
+    halo = jnp.concatenate(
+        [
+            halo[:8] + jnp.where(row == 0, y_down, 0.0),
+            halo[8 : ny - 8],
+            halo[ny - 8 :] + jnp.where(row == 7, y_up, 0.0),
+        ],
+        0,
+    )
+    new[x, :ny, :nz] = part[x] + w[x] * halo
+    beside = yu[x - 1] + yu[x + 1]
+    beside = beside + jnp.where(row == 0, pltpu.roll(u[x, ny - 8 :, :], 1, 0), y_down)
+    beside = beside + jnp.where(row == 7, pltpu.roll(u[x, :8, :], 7, 0), y_up)
+    left = jnp.where(lane_z == 0, jnp.concatenate([e_left, e_left], 1), y_left)
+    right = jnp.where(lane_z == nz - 1, jnp.concatenate([e_right, e_right], 1), y_right)
+    new[x, ny:, :nz] = 0.2 * y + yw[x] * (yr[x] + (beside + (left + right)))
+    column = jnp.concatenate([t, e], 0)
+    beside = jnp.concatenate([tu[x - 1] + tu[x + 1], eu[x - 1] + eu[x + 1]], 0)
+    beside = beside + (pltpu.roll(column, 1, 0) + pltpu.roll(column, ny + 7, 0))
+    left = [jnp.where(lane == 0, edge[x], t_left), jnp.where(lane_e == 0, y_left[:, :128], e_left)]
+    right = [jnp.where(lane == 127, edge[x], t_right), jnp.where(lane_e == 127, y_right[:, nz - 128 :], e_right)]
+    beside = beside + (jnp.concatenate(left, 0) + jnp.concatenate(right, 0))
+    r, w = jnp.concatenate([tr[x], er[x]], 0), jnp.concatenate([tw[x], ew[x]], 0)
+    new[x, :, nz:] = 0.2 * column + w * (r + beside)
+
+
+def spread_z(high, low, j):
+    tile = jnp.where(iota(high.shape, 1) // 4 == j, high, low)
+    return pltpu.roll(tile, 128 - 4 * j, 1) if j else tile
 
 
 def unpack_z(za, zb, tu, tr, tw):
@@ -228,16 +267,20 @@
 
 def centre(*refs):
     u0, r0, w0 = refs[0:4], refs[4:8], refs[8:12]
-    out, rest, ends = refs[12], refs[13], refs[14:17]
-    last, sem = refs[17:19]
-    steps = refs[19:22]
+    part, edge = refs[12:14]
+    out, rest, ends = refs[14], refs[15], refs[16:19]
+    last, sem = refs[19:21]
+    steps = refs[21:24]
     nx, ny, nz = u0[0].shape
     done, full, first, stop = steps_of(nx)
 
     def plane(k, x):
-        return whole(x, *u0) if k == 0 else steps[k - 1][x]
+        return steps[k - 1][x]
 
     def one(k, x):
+        if k == 0:
+            finish(x, u0, r0, w0, part, edge, steps[0])
+            return
         r, w = whole(x, *r0), whole(x, *w0)
         new = stencil(plane(k, x - 1), plane(k, x), plane(k, x + 1), r, w)
         if k < SWEEPS - 2:
@@ -349,16 +392,14 @@
 def shards(u, r, s):
     nx, ny, nz = u.shape
     cells = nx * ny * nz
-    raw = (u, r, s)
-    fixed = [pltpu.with_memory_space_constraint(v, pltpu.HBM) for v in raw]
-    scratch = [pltpu.VMEM((3, 2, nx, 8, nz), F32), pltpu.SemaphoreType.DMA((3, 2))]
-    sent = call(pack_y, [(3, nx // 2, 8, nz)] * 2, fixed, cells // 4, scratch, 8, hbm_in=range(3))
-    y = swap(sent, "gy")
-    sent = call(pack_z, [(3, nx // 32, ny, 128)] * 2, raw, cells)
-    z = swap(sent, "gz")
-    sent = call(pack_x, [(len(LAYERS), ny, nz)] * 2, raw, cells // 8)
-    x = swap(sent, "gx")
-    (w,) = call(weigh, [u.shape], (s,), 8 * cells)
+    raw = [pltpu.with_memory_space_constraint(v, pltpu.HBM) for v in (u, r, s)]
+    faces = [(3, nx // 2, 8, nz)] * 2 + [(3, nx // 32, ny, 128)] * 2 + [(len(LAYERS), ny, nz)] * 2
+    scratch = [pltpu.SemaphoreType.DMA((nx // CHUNK, 3))]
+    u, r, s, *sent = call(pack, [u.shape] * 3 + faces, raw, cells // 4, scratch, hbm_in=range(3))
+    y = swap(sent[0:2], "gy")
+    z = swap(sent[2:4], "gz")
+    x = swap(sent[4:6], "gx")
+    w, part, edge = call(begin, [u.shape] * 2 + [(nx, ny, 128)], (u, r, s), 20 * cells)
     sent = call(pack_yz, [(3, nx // 32, 8, 128)] * 2, z, cells // 64)
     b = swap(sent, "gy")
     t = call(unpack_z, [(nx, ny, 128)] * 3, z, 8 * cells)
@@ -372,7 +413,7 @@
     scratch = [pltpu.VMEM(u.shape, F32), pltpu.SemaphoreType.DMA] + [pltpu.VMEM((nx,) + block, F32)] * 3
     left = (nx - WIDE - stop + first - WIDE, ny, nz)
     out, rest, *ends = call(
-        centre, [u.shape, left] + [(4,) + block] * 3, parts, 60 * cells, scratch, 16, hbm_out=(0,)
+        centre, [u.shape, left] + [(4,) + block] * 3, (*parts, part, edge), 60 * cells, scratch, 16, hbm_out=(0,)
     )
     scratch = [
         pltpu.VMEM((2, len(LAYERS)) + block, F32),

time: 40.1 us -> 41.7 us (1.040)
  Pallas kernels: 16.5 us -> 18 us
    pallas_call x10 -> x8, Pallas kernels: 16.5 us -> 18 us  [call(): pl.pallas_call(kernel, out_shape=[jax.ShapeDtypeStruct(s, F32) for s in o...]
where the time goes in v3:
time: 41.7 us; the launch traced here: 41.3 us
  starting transfers between devices  18.2 us (44%)
  Pallas kernels  18 us (43%)
  waiting for transfers between devices  4.83 us (12%)
    ppermute x10, starting transfers between devices, swap(): return (lax.ppermute(sent[0], axis, near), lax.ppermute(sent[1], axis, far))  18.2 us
    pallas_call x8, Pallas kernels, call(): pl.pallas_call(kernel, out_shape=[jax.ShapeDtypeStruct(s, F32) for s in o...  18 us
    ppermute x10, waiting for transfers between devices, swap(): return (lax.ppermute(sent[0], axis, near), lax.ppermute(sent[1], axis, far))  4.83 us
  transfers between devices with their start and end apart: 10, of which 2 were waited for; matrix products, arithmetic and copies ran while one was open for 0% of the time, Pallas kernels for 31%

profile of v3, /device:TPU:1, one launch (start us, length us, event | category | flops | bytes accessed | tf_op | source)
XLA Modules:
  0.0 41.3 jit_solution(6860987736741334905)
XLA Ops:
  0.0 3.1 %shard_map.37 = (f32[64,32,256]{2,1,0:T(8,128)S(1)}, f32[64,32,256]{2,1,0:T(8,128)S(1)}, f32[64,32,256]{2,1,0:T(8,128)S(1)}, f32[3,32,8,256]{3,2,1,0:T(8,128)S(1...) custom-call(f32[64,32,256]{2,1,0:T(8,128)} %u.1, ...), custom_call_target="tpu_custom_call" | custom-call | flops 131072 | bytes 1048576 | tf_op jit(solution)/shard_map/pallas_call | solution.py:20
  3.1 3.3 %collective-permute-start = (f32[3,32,8,256]{3,2,1,0:T(8,128)S(1)}, f32[3,32,8,256]{3,2,1,0:T(8,128)S(1)}, u32[]{:S(2)}, u32[]{:S(2)}) collective-permute-start(f32[3,32,8,256]{3,2,1,0:T(8,128)S(1)} %get-tuple-element.36), channel_id=1, source_target_pairs={{0,4},{4,0},{8,12},{12,8},{16,20},{20,16},{24,28},{28,24},{32,36},... | collective-permute-start | bytes 2359304 | tf_op jit(solution)/shard_map/ppermute | solution.py:40
  6.4 0.0 collective-permute-start.1
  6.4 1.1 %collective-permute-start.2 = (f32[3,2,32,128]{3,2,1,0:T(8,128)S(1)}, f32[3,2,32,128]{3,2,1,0:T(8,128)S(1)}, u32[]{:S(2)}, u32[]{:S(2)}) collective-permute-start(f32[3,2,32,128]{3,2,1,0:T(8,128)S(1)} %get-tuple-element.39), channel_id=1, source_target_pairs={{0,1},{1,0},{2,3},{3,2},{4,5},{5,4},{6,7},{7,6},{8,9},{9,8},{10,11... | collective-permute-start | bytes 294920 | tf_op jit(solution)/shard_map/ppermute | solution.py:40
  7.5 1.3 %collective-permute-start.6 = (f32[10,32,256]{2,1,0:T(8,128)S(1)}, f32[10,32,256]{2,1,0:T(8,128)S(1)}, u32[]{:S(2)}, u32[]{:S(2)}) collective-permute-start(f32[10,32,256]{2,1,0:T(8,128)S(1)} %get-tuple-element.61), channel_id=1, source_target_pairs={{0,64},{64,0},{128,192},{192,128},{1,65},{65,1},{129,193},{193,129... | collective-permute-start | bytes 983048 | tf_op jit(solution)/shard_map/ppermute | solution.py:40
  8.8 1.9 %collective-permute-start.7 = (f32[10,32,256]{2,1,0:T(8,128)S(1)}, f32[10,32,256]{2,1,0:T(8,128)S(1)}, u32[]{:S(2)}, u32[]{:S(2)}) collective-permute-start(f32[10,32,256]{2,1,0:T(8,128)S(1)} %get-tuple-element.62), channel_id=1, source_target_pairs={{0,192},{64,128},{128,64},{192,0},{1,193},{65,129},{129,65},{193,1... | collective-permute-start | bytes 983048 | tf_op jit(solution)/shard_map/ppermute | solution.py:40
  10.7 0.0 collective-permute-done.2.za
  10.7 1.8 %collective-permute-start.3 = (f32[3,2,32,128]{3,2,1,0:T(8,128)S(1)}, f32[3,2,32,128]{3,2,1,0:T(8,128)S(1)}, u32[]{:S(2)}, u32[]{:S(2)}) collective-permute-start(f32[3,2,32,128]{3,2,1,0:T(8,128)S(1)} %get-tuple-element.40), channel_id=1, source_target_pairs={{0,3},{1,2},{2,1},{3,0},{4,7},{5,6},{6,5},{7,4},{8,11},{9,10},{10,... | collective-permute-start | bytes 294920 | tf_op jit(solution)/shard_map/ppermute | solution.py:40
  12.5 3.2 %collective-permute-done.3.zb = f32[3,2,32,128]{3,2,1,0:T(8,128)S(1)} collective-permute-done((f32[3,2,32,128]{3,2,1,0:T(8,128)S(1)}, f32[3,2,32,128]{3,2,1,0:T(8,128)S(1)}, u32[]{:S(2)}, u32[]{:S(2)}) %collective-permute-start.3) | collective-permute-done | bytes 98336 | tf_op jit(solution)/shard_map/ppermute | solution.py:40
  15.7 6.1 %collective-permute-start.4 = (f32[3,2,8,128]{3,2,1,0:T(8,128)S(1)}, f32[3,2,8,128]{3,2,1,0:T(8,128)S(1)}, u32[]{:S(2)}, u32[]{:S(2)}) collective-permute-start(f32[3,2,8,128]{3,2,1,0:T(8,128)S(1)} %get-tuple-element.42), channel_id=1, source_target_pairs={{0,4},{4,0},{8,12},{12,8},{16,20},{20,16},{24,28},{28,24},{32,36},... | collective-permute-start | bytes 73736 | tf_op jit(solution)/shard_map/ppermute | solution.py:40
  21.8 0.0 collective-permute-done.near
  21.8 0.0 collective-permute-start.5
  21.8 1.2 %shard_map.39 = (f32[64,32,128]{2,1,0:T(8,128)S(1)}, f32[64,32,128]{2,1,0:T(8,128)S(1)}, f32[64,32,128]{2,1,0:T(8,128)S(1)}) custom-call(f32[3,2,32,128]{3,2,1,0:T(8,128)S(1)} %collective-permute-done.2.za, f32[3,2,32,128]{3,2,1,0:T(8,128)S(1)} %collective-permute-done.3.zb), custom_call_target="tpu_custom_call" | custom-call | flops 4194304 | bytes 1048576 | tf_op jit(solution)/shard_map/pallas_call | solution.py:20
  23.1 0.0 collective-permute-done.1.far
  23.1 0.3 shard_map.38
  23.4 0.0 collective-permute-done.4.b_near
  23.4 1.7 %collective-permute-done.5.b_far = f32[3,2,8,128]{3,2,1,0:T(8,128)S(1)} collective-permute-done((f32[3,2,8,128]{3,2,1,0:T(8,128)S(1)}, f32[3,2,8,128]{3,2,1,0:T(8,128)S(1)}, u32[]{:S(2)}, u32[]{:S(2)}) %collective-permute-start.5) | collective-permute-done | bytes 24608 | tf_op jit(solution)/shard_map/ppermute | solution.py:40
  25.1 0.4 %shard_map.41 = (f32[64,8,128]{2,1,0:T(8,128)S(1)}, f32[64,8,128]{2,1,0:T(8,128)S(1)}, f32[64,8,128]{2,1,0:T(8,128)S(1)}, f32[13,8,256]{2,1,0:T(8,128)S(1)}, f32[13,8,256]{2,1,0:T(8,128)S(1)}) custom-call(f32[3,2,8,128]{3,2,1,0:T(8,128)S(1)} %collective-permute-done.4.b_near, f32[3,2,8,128]{3,2,1,0:T(8,128)S(1)} %collective-permute-done.5.b_far, ...), custom_call_target="tpu_custom_call" | custom-call | flops 65536 | bytes 1048576 | tf_op jit(solution)/shard_map/pallas_call | solution.py:20
  25.5 0.7 %collective-permute-start.8 = (f32[13,8,256]{2,1,0:T(8,128)S(1)}, f32[13,8,256]{2,1,0:T(8,128)S(1)}, u32[]{:S(2)}, u32[]{:S(2)}) collective-permute-start(f32[13,8,256]{2,1,0:T(8,128)S(1)} %get-tuple-element.63), channel_id=1, source_target_pairs={{0,64},{64,0},{128,192},{192,128},{1,65},{65,1},{129,193},{193,129... | collective-permute-start | bytes 319496 | tf_op jit(solution)/shard_map/ppermute | solution.py:40
  26.3 1.9 %collective-permute-start.9 = (f32[13,8,256]{2,1,0:T(8,128)S(1)}, f32[13,8,256]{2,1,0:T(8,128)S(1)}, u32[]{:S(2)}, u32[]{:S(2)}) collective-permute-start(f32[13,8,256]{2,1,0:T(8,128)S(1)} %get-tuple-element.64), channel_id=1, source_target_pairs={{0,192},{64,128},{128,64},{192,0},{1,193},{65,129},{129,65},{193,1... | collective-permute-start | bytes 319496 | tf_op jit(solution)/shard_map/ppermute | solution.py:40
  28.2 3.5 %shard_map.42 = (f32[64,32,256]{2,1,0:T(8,128)S(1)}, f32[64,32,256]{2,1,0:T(8,128)S(1)}, f32[64,32,128]{2,1,0:T(8,128)S(1)}) custom-call(f32[64,32,256]{2,1,0:T(8,128)S(1)} %get-tuple-element.35.u.refs_0_, f32[64,32,256]{2,1,0:T(8,128)S(1)} %get-tuple-element.49.r.refs_4_, f32[64,32,256]{2,1,0:T(8,128)S(1)} %get-tuple-element.51.s), custom_call_target="tpu_custom_call" | custom-call | flops 10485760 | bytes 1048576 | tf_op jit(solution)/shard_map/pallas_call | solution.py:20
  31.6 7.4 %shard_map.43 = (f32[64,32,256]{2,1,0:T(8,128)}, f32[16,32,256]{2,1,0:T(8,128)S(1)}, f32[4,40,384]{2,1,0:T(8,128)S(1)}, f32[4,40,384]{2,1,0:T(8,128)S(1)}, f32[4,40,384]{2,1,0:T(8,128)S(1)}) custom-call(f32[64,32,256]{2,1,0:T(8,128)S(1)} %get-tuple-element.35.u.refs_0_, f32[64,8,256]{2,1,0:T(8,128)S(1)} %get-tuple-element.38.yu.refs_1_, ...), custom_call_target="tpu_custom_call" | custom-call | flops 31457280 | bytes 1048576 | tf_op jit(solution)/shard_map/pallas_call | solution.py:20
  39.1 0.0 collective-permute-done.6.refs_17_
  39.1 0.0 collective-permute-done.7.refs_18_
  39.1 0.0 collective-permute-done.8.refs_19_
  39.1 0.0 collective-permute-done.9.refs_20_
  39.1 2.0 %shard_map.44 = f32[64,32,256]{2,1,0:T(8,128)} custom-call(f32[64,32,256]{2,1,0:T(8,128)S(1)} %get-tuple-element.35.u.refs_0_, f32[64,8,256]{2,1,0:T(8,128)S(1)} %get-tuple-element.38.yu.refs_1_, f32[64,32,128]{2,1,0:T(8,128)S(1)} %get-tuple-element.41.tu.refs_2_, f32[64,8,128]{2,1,0:T(8,128)S(1)} %get-tuple-element.48.refs_3_, ...), custom_call_target="tpu_custom_call", output_to_operand_aliasing={{}: (12, {})} | custom-call | flops 4194304 | bytes 1048576 | tf_op jit(solution)/shard_map/pallas_call | solution.py:20
  (1 shorter events, 0.0 us)
Async XLA Ops:
  3.1 18.7 %collective-permute-start = (f32[3,32,8,256]{3,2,1,0:T(8,128)S(1)}, f32[3,32,8,256]{3,2,1,0:T(8,128)S(1)}, u32[]{:S(2)}, u32[]{:S(2)}) collective-permute-start(f32[3,32,8,256]{3,2,1,0:T(8,128)S(1)} %get-tuple-element.36), channel_id=1, source_target_pairs={{0,4},{4,0},{8,12},{12,8},{16,20},{20,16},{24,28},{28,24},{32,36},... | collective-permute-start | bytes 2359304 | tf_op jit(solution)/shard_map/ppermute | solution.py:40
  6.4 16.7 %collective-permute-start.1 = (f32[3,32,8,256]{3,2,1,0:T(8,128)S(1)}, f32[3,32,8,256]{3,2,1,0:T(8,128)S(1)}, u32[]{:S(2)}, u32[]{:S(2)}) collective-permute-start(f32[3,32,8,256]{3,2,1,0:T(8,128)S(1)} %get-tuple-element.37), channel_id=1, source_target_pairs={{0,60},{4,8},{8,4},{12,16},{16,12},{20,24},{24,20},{28,32},{32,28}... | collective-permute-start | bytes 2359304 | tf_op jit(solution)/shard_map/ppermute | solution.py:40
  6.4 4.3 %collective-permute-start.2 = (f32[3,2,32,128]{3,2,1,0:T(8,128)S(1)}, f32[3,2,32,128]{3,2,1,0:T(8,128)S(1)}, u32[]{:S(2)}, u32[]{:S(2)}) collective-permute-start(f32[3,2,32,128]{3,2,1,0:T(8,128)S(1)} %get-tuple-element.39), channel_id=1, source_target_pairs={{0,1},{1,0},{2,3},{3,2},{4,5},{5,4},{6,7},{7,6},{8,9},{9,8},{10,11... | collective-permute-start | bytes 294920 | tf_op jit(solution)/shard_map/ppermute | solution.py:40
  7.5 31.6 %collective-permute-start.6 = (f32[10,32,256]{2,1,0:T(8,128)S(1)}, f32[10,32,256]{2,1,0:T(8,128)S(1)}, u32[]{:S(2)}, u32[]{:S(2)}) collective-permute-start(f32[10,32,256]{2,1,0:T(8,128)S(1)} %get-tuple-element.61), channel_id=1, source_target_pairs={{0,64},{64,0},{128,192},{192,128},{1,65},{65,1},{129,193},{193,129... | collective-permute-start | bytes 983048 | tf_op jit(solution)/shard_map/ppermute | solution.py:40
  8.8 30.3 %collective-permute-start.7 = (f32[10,32,256]{2,1,0:T(8,128)S(1)}, f32[10,32,256]{2,1,0:T(8,128)S(1)}, u32[]{:S(2)}, u32[]{:S(2)}) collective-permute-start(f32[10,32,256]{2,1,0:T(8,128)S(1)} %get-tuple-element.62), channel_id=1, source_target_pairs={{0,192},{64,128},{128,64},{192,0},{1,193},{65,129},{129,65},{193,1... | collective-permute-start | bytes 983048 | tf_op jit(solution)/shard_map/ppermute | solution.py:40
  10.7 5.0 %collective-permute-start.3 = (f32[3,2,32,128]{3,2,1,0:T(8,128)S(1)}, f32[3,2,32,128]{3,2,1,0:T(8,128)S(1)}, u32[]{:S(2)}, u32[]{:S(2)}) collective-permute-start(f32[3,2,32,128]{3,2,1,0:T(8,128)S(1)} %get-tuple-element.40), channel_id=1, source_target_pairs={{0,3},{1,2},{2,1},{3,0},{4,7},{5,6},{6,5},{7,4},{8,11},{9,10},{10,... | collective-permute-start | bytes 294920 | tf_op jit(solution)/shard_map/ppermute | solution.py:40
  15.7 7.7 %collective-permute-start.4 = (f32[3,2,8,128]{3,2,1,0:T(8,128)S(1)}, f32[3,2,8,128]{3,2,1,0:T(8,128)S(1)}, u32[]{:S(2)}, u32[]{:S(2)}) collective-permute-start(f32[3,2,8,128]{3,2,1,0:T(8,128)S(1)} %get-tuple-element.42), channel_id=1, source_target_pairs={{0,4},{4,0},{8,12},{12,8},{16,20},{20,16},{24,28},{28,24},{32,36},... | collective-permute-start | bytes 73736 | tf_op jit(solution)/shard_map/ppermute | solution.py:40
  21.8 3.3 %collective-permute-start.5 = (f32[3,2,8,128]{3,2,1,0:T(8,128)S(1)}, f32[3,2,8,128]{3,2,1,0:T(8,128)S(1)}, u32[]{:S(2)}, u32[]{:S(2)}) collective-permute-start(f32[3,2,8,128]{3,2,1,0:T(8,128)S(1)} %get-tuple-element.43), channel_id=1, source_target_pairs={{0,60},{4,8},{8,4},{12,16},{16,12},{20,24},{24,20},{28,32},{32,28}... | collective-permute-start | bytes 73736 | tf_op jit(solution)/shard_map/ppermute | solution.py:40
  25.5 13.6 %collective-permute-start.8 = (f32[13,8,256]{2,1,0:T(8,128)S(1)}, f32[13,8,256]{2,1,0:T(8,128)S(1)}, u32[]{:S(2)}, u32[]{:S(2)}) collective-permute-start(f32[13,8,256]{2,1,0:T(8,128)S(1)} %get-tuple-element.63), channel_id=1, source_target_pairs={{0,64},{64,0},{128,192},{192,128},{1,65},{65,1},{129,193},{193,129... | collective-permute-start | bytes 319496 | tf_op jit(solution)/shard_map/ppermute | solution.py:40
  26.3 12.8 %collective-permute-start.9 = (f32[13,8,256]{2,1,0:T(8,128)S(1)}, f32[13,8,256]{2,1,0:T(8,128)S(1)}, u32[]{:S(2)}, u32[]{:S(2)}) collective-permute-start(f32[13,8,256]{2,1,0:T(8,128)S(1)} %get-tuple-element.64), channel_id=1, source_target_pairs={{0,192},{64,128},{128,64},{192,0},{1,193},{65,129},{129,65},{193,1... | collective-permute-start | bytes 319496 | tf_op jit(solution)/shard_map/ppermute | solution.py:40

commit v4 on v3

--- a/solution.py
+++ b/solution.py
@@ -116,13 +116,12 @@
     nx, ny, nz = u.shape
     row, lane = iota((ny, nz), 0), iota((ny, nz), 1)
     half = iota((ny, 128), 1) < 64
-    w[0] = weight(s[0])
-    w[nx - 1] = weight(s[nx - 1])
 
     def body(i, c):
-        for x in (1 + 2 * i, 2 + 2 * i):
+        for j in range(8):
+            x = 8 * i + j
             here = u[x]
-            beside = u[x - 1] + u[x + 1]
+            beside = u[jnp.maximum(x - 1, 0)] + u[jnp.minimum(x + 1, nx - 1)]
             beside = beside + jnp.where(row == 0, 0.0, pltpu.roll(here, 1, 0))
             beside = beside + jnp.where(row == ny - 1, 0.0, pltpu.roll(here, ny - 1, 0))
             left, right = pltpu.roll(here, 1, 1), pltpu.roll(here, nz - 1, 1)
@@ -133,7 +132,7 @@
             part[x] = 0.2 * here + here_w * (r[x] + beside)
         return c
 
-    lax.fori_loop(0, (nx - 2) // 2, body, 0)
+    lax.fori_loop(0, nx // 8, body, 0)
 
 
 def finish(x, u0, r0, w0, part, edge, new):

time: 41.7 us -> 40.1 us (0.962)
  Pallas kernels: 18 us -> 16.4 us
    pallas_call x8, Pallas kernels: 18 us -> 16.4 us  [call(): pl.pallas_call(kernel, out_shape=[jax.ShapeDtypeStruct(s, F32) for s in o...]
  transfers between devices with their start and end apart: 10 -> 10, of which waited for: 2 -> 2; matrix products, arithmetic and copies ran while one was open for 0% -> 0% of each run, Pallas kernels for 31% -> 28%
where the time goes in v4:
time: 40.1 us; the launch traced here: 39.7 us
  starting transfers between devices  18.2 us (45%)
  Pallas kernels  16.4 us (41%)
  waiting for transfers between devices  4.83 us (12%)
    ppermute x10, starting transfers between devices, swap(): return (lax.ppermute(sent[0], axis, near), lax.ppermute(sent[1], axis, far))  18.2 us
    pallas_call x8, Pallas kernels, call(): pl.pallas_call(kernel, out_shape=[jax.ShapeDtypeStruct(s, F32) for s in o...  16.4 us
    ppermute x10, waiting for transfers between devices, swap(): return (lax.ppermute(sent[0], axis, near), lax.ppermute(sent[1], axis, far))  4.83 us
  transfers between devices with their start and end apart: 10, of which 2 were waited for; matrix products, arithmetic and copies ran while one was open for 0% of the time, Pallas kernels for 28%

profile of v4, /device:TPU:1, one launch (start us, length us, event | category | flops | bytes accessed | tf_op | source)
XLA Modules:
  0.0 39.7 jit_solution(10278397809349767685)
XLA Ops:
  0.0 3.1 %shard_map.37 = (f32[64,32,256]{2,1,0:T(8,128)S(1)}, f32[64,32,256]{2,1,0:T(8,128)S(1)}, f32[64,32,256]{2,1,0:T(8,128)S(1)}, f32[3,32,8,256]{3,2,1,0:T(8,128)S(1...) custom-call(f32[64,32,256]{2,1,0:T(8,128)} %u.1, ...), custom_call_target="tpu_custom_call" | custom-call | flops 131072 | bytes 1048576 | tf_op jit(solution)/shard_map/pallas_call | solution.py:20
  3.1 3.3 %collective-permute-start = (f32[3,32,8,256]{3,2,1,0:T(8,128)S(1)}, f32[3,32,8,256]{3,2,1,0:T(8,128)S(1)}, u32[]{:S(2)}, u32[]{:S(2)}) collective-permute-start(f32[3,32,8,256]{3,2,1,0:T(8,128)S(1)} %get-tuple-element.36), channel_id=1, source_target_pairs={{0,4},{4,0},{8,12},{12,8},{16,20},{20,16},{24,28},{28,24},{32,36},... | collective-permute-start | bytes 2359304 | tf_op jit(solution)/shard_map/ppermute | solution.py:40
  6.4 0.0 collective-permute-start.1
  6.4 1.1 %collective-permute-start.2 = (f32[3,2,32,128]{3,2,1,0:T(8,128)S(1)}, f32[3,2,32,128]{3,2,1,0:T(8,128)S(1)}, u32[]{:S(2)}, u32[]{:S(2)}) collective-permute-start(f32[3,2,32,128]{3,2,1,0:T(8,128)S(1)} %get-tuple-element.39), channel_id=1, source_target_pairs={{0,1},{1,0},{2,3},{3,2},{4,5},{5,4},{6,7},{7,6},{8,9},{9,8},{10,11... | collective-permute-start | bytes 294920 | tf_op jit(solution)/shard_map/ppermute | solution.py:40
  7.5 1.3 %collective-permute-start.6 = (f32[10,32,256]{2,1,0:T(8,128)S(1)}, f32[10,32,256]{2,1,0:T(8,128)S(1)}, u32[]{:S(2)}, u32[]{:S(2)}) collective-permute-start(f32[10,32,256]{2,1,0:T(8,128)S(1)} %get-tuple-element.61), channel_id=1, source_target_pairs={{0,64},{64,0},{128,192},{192,128},{1,65},{65,1},{129,193},{193,129... | collective-permute-start | bytes 983048 | tf_op jit(solution)/shard_map/ppermute | solution.py:40
  8.8 1.9 %collective-permute-start.7 = (f32[10,32,256]{2,1,0:T(8,128)S(1)}, f32[10,32,256]{2,1,0:T(8,128)S(1)}, u32[]{:S(2)}, u32[]{:S(2)}) collective-permute-start(f32[10,32,256]{2,1,0:T(8,128)S(1)} %get-tuple-element.62), channel_id=1, source_target_pairs={{0,192},{64,128},{128,64},{192,0},{1,193},{65,129},{129,65},{193,1... | collective-permute-start | bytes 983048 | tf_op jit(solution)/shard_map/ppermute | solution.py:40
  10.7 0.0 collective-permute-done.2.za
  10.7 1.8 %collective-permute-start.3 = (f32[3,2,32,128]{3,2,1,0:T(8,128)S(1)}, f32[3,2,32,128]{3,2,1,0:T(8,128)S(1)}, u32[]{:S(2)}, u32[]{:S(2)}) collective-permute-start(f32[3,2,32,128]{3,2,1,0:T(8,128)S(1)} %get-tuple-element.40), channel_id=1, source_target_pairs={{0,3},{1,2},{2,1},{3,0},{4,7},{5,6},{6,5},{7,4},{8,11},{9,10},{10,... | collective-permute-start | bytes 294920 | tf_op jit(solution)/shard_map/ppermute | solution.py:40
  12.5 3.2 %collective-permute-done.3.zb = f32[3,2,32,128]{3,2,1,0:T(8,128)S(1)} collective-permute-done((f32[3,2,32,128]{3,2,1,0:T(8,128)S(1)}, f32[3,2,32,128]{3,2,1,0:T(8,128)S(1)}, u32[]{:S(2)}, u32[]{:S(2)}) %collective-permute-start.3) | collective-permute-done | bytes 98336 | tf_op jit(solution)/shard_map/ppermute | solution.py:40
  15.7 6.1 %collective-permute-start.4 = (f32[3,2,8,128]{3,2,1,0:T(8,128)S(1)}, f32[3,2,8,128]{3,2,1,0:T(8,128)S(1)}, u32[]{:S(2)}, u32[]{:S(2)}) collective-permute-start(f32[3,2,8,128]{3,2,1,0:T(8,128)S(1)} %get-tuple-element.42), channel_id=1, source_target_pairs={{0,4},{4,0},{8,12},{12,8},{16,20},{20,16},{24,28},{28,24},{32,36},... | collective-permute-start | bytes 73736 | tf_op jit(solution)/shard_map/ppermute | solution.py:40
  21.8 0.0 collective-permute-done.near
  21.8 0.0 collective-permute-start.5
  21.8 1.2 %shard_map.39 = (f32[64,32,128]{2,1,0:T(8,128)S(1)}, f32[64,32,128]{2,1,0:T(8,128)S(1)}, f32[64,32,128]{2,1,0:T(8,128)S(1)}) custom-call(f32[3,2,32,128]{3,2,1,0:T(8,128)S(1)} %collective-permute-done.2.za, f32[3,2,32,128]{3,2,1,0:T(8,128)S(1)} %collective-permute-done.3.zb), custom_call_target="tpu_custom_call" | custom-call | flops 4194304 | bytes 1048576 | tf_op jit(solution)/shard_map/pallas_call | solution.py:20
  23.1 0.0 collective-permute-done.1.far
  23.1 0.3 shard_map.38
  23.4 0.0 collective-permute-done.4.b_near
  23.4 1.7 %collective-permute-done.5.b_far = f32[3,2,8,128]{3,2,1,0:T(8,128)S(1)} collective-permute-done((f32[3,2,8,128]{3,2,1,0:T(8,128)S(1)}, f32[3,2,8,128]{3,2,1,0:T(8,128)S(1)}, u32[]{:S(2)}, u32[]{:S(2)}) %collective-permute-start.5) | collective-permute-done | bytes 24608 | tf_op jit(solution)/shard_map/ppermute | solution.py:40
  25.1 0.4 %shard_map.41 = (f32[64,8,128]{2,1,0:T(8,128)S(1)}, f32[64,8,128]{2,1,0:T(8,128)S(1)}, f32[64,8,128]{2,1,0:T(8,128)S(1)}, f32[13,8,256]{2,1,0:T(8,128)S(1)}, f32[13,8,256]{2,1,0:T(8,128)S(1)}) custom-call(f32[3,2,8,128]{3,2,1,0:T(8,128)S(1)} %collective-permute-done.4.b_near, f32[3,2,8,128]{3,2,1,0:T(8,128)S(1)} %collective-permute-done.5.b_far, ...), custom_call_target="tpu_custom_call" | custom-call | flops 65536 | bytes 1048576 | tf_op jit(solution)/shard_map/pallas_call | solution.py:20
  25.5 0.7 %collective-permute-start.8 = (f32[13,8,256]{2,1,0:T(8,128)S(1)}, f32[13,8,256]{2,1,0:T(8,128)S(1)}, u32[]{:S(2)}, u32[]{:S(2)}) collective-permute-start(f32[13,8,256]{2,1,0:T(8,128)S(1)} %get-tuple-element.63), channel_id=1, source_target_pairs={{0,64},{64,0},{128,192},{192,128},{1,65},{65,1},{129,193},{193,129... | collective-permute-start | bytes 319496 | tf_op jit(solution)/shard_map/ppermute | solution.py:40
  26.3 1.9 %collective-permute-start.9 = (f32[13,8,256]{2,1,0:T(8,128)S(1)}, f32[13,8,256]{2,1,0:T(8,128)S(1)}, u32[]{:S(2)}, u32[]{:S(2)}) collective-permute-start(f32[13,8,256]{2,1,0:T(8,128)S(1)} %get-tuple-element.64), channel_id=1, source_target_pairs={{0,192},{64,128},{128,64},{192,0},{1,193},{65,129},{129,65},{193,1... | collective-permute-start | bytes 319496 | tf_op jit(solution)/shard_map/ppermute | solution.py:40
  28.2 1.9 %shard_map.42 = (f32[64,32,256]{2,1,0:T(8,128)S(1)}, f32[64,32,256]{2,1,0:T(8,128)S(1)}, f32[64,32,128]{2,1,0:T(8,128)S(1)}) custom-call(f32[64,32,256]{2,1,0:T(8,128)S(1)} %get-tuple-element.35.u.refs_0_, f32[64,32,256]{2,1,0:T(8,128)S(1)} %get-tuple-element.49.r.refs_4_, f32[64,32,256]{2,1,0:T(8,128)S(1)} %get-tuple-element.51.s), custom_call_target="tpu_custom_call" | custom-call | flops 10485760 | bytes 1048576 | tf_op jit(solution)/shard_map/pallas_call | solution.py:20
  30.1 7.4 %shard_map.43 = (f32[64,32,256]{2,1,0:T(8,128)}, f32[16,32,256]{2,1,0:T(8,128)S(1)}, f32[4,40,384]{2,1,0:T(8,128)S(1)}, f32[4,40,384]{2,1,0:T(8,128)S(1)}, f32[4,40,384]{2,1,0:T(8,128)S(1)}) custom-call(f32[64,32,256]{2,1,0:T(8,128)S(1)} %get-tuple-element.35.u.refs_0_, f32[64,8,256]{2,1,0:T(8,128)S(1)} %get-tuple-element.38.yu.refs_1_, ...), custom_call_target="tpu_custom_call" | custom-call | flops 31457280 | bytes 1048576 | tf_op jit(solution)/shard_map/pallas_call | solution.py:20
  37.5 0.0 collective-permute-done.6.refs_17_
  37.5 0.0 collective-permute-done.7.refs_18_
  37.5 0.0 collective-permute-done.8.refs_19_
  37.5 0.0 collective-permute-done.9.refs_20_
  37.5 2.0 %shard_map.44 = f32[64,32,256]{2,1,0:T(8,128)} custom-call(f32[64,32,256]{2,1,0:T(8,128)S(1)} %get-tuple-element.35.u.refs_0_, f32[64,8,256]{2,1,0:T(8,128)S(1)} %get-tuple-element.38.yu.refs_1_, f32[64,32,128]{2,1,0:T(8,128)S(1)} %get-tuple-element.41.tu.refs_2_, f32[64,8,128]{2,1,0:T(8,128)S(1)} %get-tuple-element.48.refs_3_, ...), custom_call_target="tpu_custom_call", output_to_operand_aliasing={{}: (12, {})} | custom-call | flops 4194304 | bytes 1048576 | tf_op jit(solution)/shard_map/pallas_call | solution.py:20
  (1 shorter events, 0.0 us)
Async XLA Ops:
  3.1 18.7 %collective-permute-start = (f32[3,32,8,256]{3,2,1,0:T(8,128)S(1)}, f32[3,32,8,256]{3,2,1,0:T(8,128)S(1)}, u32[]{:S(2)}, u32[]{:S(2)}) collective-permute-start(f32[3,32,8,256]{3,2,1,0:T(8,128)S(1)} %get-tuple-element.36), channel_id=1, source_target_pairs={{0,4},{4,0},{8,12},{12,8},{16,20},{20,16},{24,28},{28,24},{32,36},... | collective-permute-start | bytes 2359304 | tf_op jit(solution)/shard_map/ppermute | solution.py:40
  6.4 16.7 %collective-permute-start.1 = (f32[3,32,8,256]{3,2,1,0:T(8,128)S(1)}, f32[3,32,8,256]{3,2,1,0:T(8,128)S(1)}, u32[]{:S(2)}, u32[]{:S(2)}) collective-permute-start(f32[3,32,8,256]{3,2,1,0:T(8,128)S(1)} %get-tuple-element.37), channel_id=1, source_target_pairs={{0,60},{4,8},{8,4},{12,16},{16,12},{20,24},{24,20},{28,32},{32,28}... | collective-permute-start | bytes 2359304 | tf_op jit(solution)/shard_map/ppermute | solution.py:40
  6.4 4.3 %collective-permute-start.2 = (f32[3,2,32,128]{3,2,1,0:T(8,128)S(1)}, f32[3,2,32,128]{3,2,1,0:T(8,128)S(1)}, u32[]{:S(2)}, u32[]{:S(2)}) collective-permute-start(f32[3,2,32,128]{3,2,1,0:T(8,128)S(1)} %get-tuple-element.39), channel_id=1, source_target_pairs={{0,1},{1,0},{2,3},{3,2},{4,5},{5,4},{6,7},{7,6},{8,9},{9,8},{10,11... | collective-permute-start | bytes 294920 | tf_op jit(solution)/shard_map/ppermute | solution.py:40
  7.5 30.0 %collective-permute-start.6 = (f32[10,32,256]{2,1,0:T(8,128)S(1)}, f32[10,32,256]{2,1,0:T(8,128)S(1)}, u32[]{:S(2)}, u32[]{:S(2)}) collective-permute-start(f32[10,32,256]{2,1,0:T(8,128)S(1)} %get-tuple-element.61), channel_id=1, source_target_pairs={{0,64},{64,0},{128,192},{192,128},{1,65},{65,1},{129,193},{193,129... | collective-permute-start | bytes 983048 | tf_op jit(solution)/shard_map/ppermute | solution.py:40
  8.8 28.7 %collective-permute-start.7 = (f32[10,32,256]{2,1,0:T(8,128)S(1)}, f32[10,32,256]{2,1,0:T(8,128)S(1)}, u32[]{:S(2)}, u32[]{:S(2)}) collective-permute-start(f32[10,32,256]{2,1,0:T(8,128)S(1)} %get-tuple-element.62), channel_id=1, source_target_pairs={{0,192},{64,128},{128,64},{192,0},{1,193},{65,129},{129,65},{193,1... | collective-permute-start | bytes 983048 | tf_op jit(solution)/shard_map/ppermute | solution.py:40
  10.7 5.0 %collective-permute-start.3 = (f32[3,2,32,128]{3,2,1,0:T(8,128)S(1)}, f32[3,2,32,128]{3,2,1,0:T(8,128)S(1)}, u32[]{:S(2)}, u32[]{:S(2)}) collective-permute-start(f32[3,2,32,128]{3,2,1,0:T(8,128)S(1)} %get-tuple-element.40), channel_id=1, source_target_pairs={{0,3},{1,2},{2,1},{3,0},{4,7},{5,6},{6,5},{7,4},{8,11},{9,10},{10,... | collective-permute-start | bytes 294920 | tf_op jit(solution)/shard_map/ppermute | solution.py:40
  15.7 7.7 %collective-permute-start.4 = (f32[3,2,8,128]{3,2,1,0:T(8,128)S(1)}, f32[3,2,8,128]{3,2,1,0:T(8,128)S(1)}, u32[]{:S(2)}, u32[]{:S(2)}) collective-permute-start(f32[3,2,8,128]{3,2,1,0:T(8,128)S(1)} %get-tuple-element.42), channel_id=1, source_target_pairs={{0,4},{4,0},{8,12},{12,8},{16,20},{20,16},{24,28},{28,24},{32,36},... | collective-permute-start | bytes 73736 | tf_op jit(solution)/shard_map/ppermute | solution.py:40
  21.8 3.3 %collective-permute-start.5 = (f32[3,2,8,128]{3,2,1,0:T(8,128)S(1)}, f32[3,2,8,128]{3,2,1,0:T(8,128)S(1)}, u32[]{:S(2)}, u32[]{:S(2)}) collective-permute-start(f32[3,2,8,128]{3,2,1,0:T(8,128)S(1)} %get-tuple-element.43), channel_id=1, source_target_pairs={{0,60},{4,8},{8,4},{12,16},{16,12},{20,24},{24,20},{28,32},{32,28}... | collective-permute-start | bytes 73736 | tf_op jit(solution)/shard_map/ppermute | solution.py:40
  25.5 12.0 %collective-permute-start.8 = (f32[13,8,256]{2,1,0:T(8,128)S(1)}, f32[13,8,256]{2,1,0:T(8,128)S(1)}, u32[]{:S(2)}, u32[]{:S(2)}) collective-permute-start(f32[13,8,256]{2,1,0:T(8,128)S(1)} %get-tuple-element.63), channel_id=1, source_target_pairs={{0,64},{64,0},{128,192},{192,128},{1,65},{65,1},{129,193},{193,129... | collective-permute-start | bytes 319496 | tf_op jit(solution)/shard_map/ppermute | solution.py:40
  26.3 11.2 %collective-permute-start.9 = (f32[13,8,256]{2,1,0:T(8,128)S(1)}, f32[13,8,256]{2,1,0:T(8,128)S(1)}, u32[]{:S(2)}, u32[]{:S(2)}) collective-permute-start(f32[13,8,256]{2,1,0:T(8,128)S(1)} %get-tuple-element.64), channel_id=1, source_target_pairs={{0,192},{64,128},{128,64},{192,0},{1,193},{65,129},{129,65},{193,1... | collective-permute-start | bytes 319496 | tf_op jit(solution)/shard_map/ppermute | solution.py:40

commit v5 on v4

--- a/solution.py
+++ b/solution.py
@@ -37,7 +37,8 @@
     n = lax.axis_size(axis)
     near = [(i, i ^ 1) for i in range(n)]
     far = [(i, (i + (1 if i % 2 else -1)) % n) for i in range(n)]
-    return lax.ppermute(sent[0], axis, near), lax.ppermute(sent[1], axis, far)
+    got = lax.ppermute(sent[1], axis, far)
+    return lax.ppermute(sent[0], axis, near), got
 
 
 def iota(shape, dim):
@@ -53,6 +54,25 @@
 def unfold(above, below):
     head = iota(above.shape, 0) < 4
     return jnp.where(head, above, below), pltpu.roll(jnp.where(head, below, above), 4, 0)
+
+
+def turn(tile, n):
+    return pltpu.roll(tile, n % 8, 0) if n % 8 else tile
+
+
+def fold_rows(held, x, at):
+    row = iota((8, held[0].shape[2]), 0)
+    tiles, rest = [], None
+    for k in range(4):
+        u, r, s = (ref[x + k, at : at + 8, :] for ref in held)
+        if at == 0:
+            tiles.append(jnp.where(row < 4, u, jnp.where(row < 7, turn(r, 4), turn(s, 7))))
+            two = turn(s, 2 * k - 1)
+        else:
+            tiles.append(jnp.where(row > 3, u, jnp.where(row > 0, turn(r, 4), turn(s, 1))))
+            two = turn(s, 2 * k - 5)
+        rest = two if k == 0 else jnp.where(row // 2 == k, two, rest)
+    return tiles + [rest]
 
 
 def pack(u, r, s, u_v, r_v, s_v, y_near, y_far, z_near, z_far, x_near, x_far, sem):
@@ -70,10 +90,6 @@
     for c in range(nx // CHUNK):
         for a, ref in enumerate(held):
             copies[c, a].wait()
-            for face, low in ((y_near, y_odd), (y_far, jnp.logical_not(y_odd))):
-                rows = pl.ds(pl.multiple_of(jnp.where(low, 0, ny - 8), 8), 8)
-                for i in range(c * CHUNK // 2, (c + 1) * CHUNK // 2):
-                    face[a, i] = fold(ref[2 * i, rows, :], ref[2 * i + 1, rows, :], low)
             g = c * CHUNK // 32
             first = c * CHUNK % 32 == 0
             low = jnp.zeros((ny, 128), F32) if first else z_near[a, g]
@@ -87,6 +103,11 @@
                 high = jnp.where(block == (j - 1) % 32, both, high)
             z_near[a, g] = jnp.where(z_odd, low, high)
             z_far[a, g] = jnp.where(z_odd, high, low)
+        for i in range(c * CHUNK // 4, (c + 1) * CHUNK // 4):
+            low, high = fold_rows(held, 4 * i, 0), fold_rows(held, 4 * i, ny - 8)
+            for n in range(5):
+                y_near[i, n] = jnp.where(y_odd, low[n], high[n])
+                y_far[i, n] = jnp.where(y_odd, high[n], low[n])
     for face, low in ((x_near, x_odd), (x_far, jnp.logical_not(x_odd))):
         for q, (a, k) in enumerate(LAYERS):
             layers = WIDE if a == 0 else WIDE - 1
@@ -193,17 +214,24 @@
 
 def unpack_y(near, far, yu, yr, yw):
     is_odd = odd("gy") == 1
-    for a, out in enumerate((yu, yr, yw)):
-
-        def body(i, c, a=a, out=out):
-            one, two = near[a, i], far[a, i]
-            above, below = jnp.where(is_odd, two, one), jnp.where(is_odd, one, two)
-            first, second = unfold(above, below)
-            out[2 * i] = weight(first) if a == 2 else first
-            out[2 * i + 1] = weight(second) if a == 2 else second
-            return c
-
-        lax.fori_loop(0, near.shape[1], body, 0, unroll=4)
+    row = iota(near.shape[2:], 0)
+
+    def body(i, c):
+        def halves(n):
+            one, two = near[i, n], far[i, n]
+            return jnp.where(is_odd, two, one), jnp.where(is_odd, one, two)
+
+        rest_above, rest_below = halves(4)
+        for k in range(4):
+            above, below = halves(k)
+            yu[4 * i + k] = jnp.where(row < 4, above, below)
+            yr[4 * i + k] = turn(jnp.where(row < 4, below, above), 4)
+            s = jnp.where(row < 4, turn(rest_above, 1 - 2 * k), turn(rest_below, 5 - 2 * k))
+            s = jnp.where(row == 0, turn(above, 1), jnp.where(row == 7, turn(below, 7), s))
+            yw[4 * i + k] = weight(s)
+        return c
+
+    lax.fori_loop(0, near.shape[0], body, 0, unroll=2)
 
 
 def pack_edges(b_near, b_far, yu, yr, yw, tu, tr, tw, eu, er, ew, near, far):
@@ -392,7 +420,7 @@
     nx, ny, nz = u.shape
     cells = nx * ny * nz
     raw = [pltpu.with_memory_space_constraint(v, pltpu.HBM) for v in (u, r, s)]
-    faces = [(3, nx // 2, 8, nz)] * 2 + [(3, nx // 32, ny, 128)] * 2 + [(len(LAYERS), ny, nz)] * 2
+    faces = [(nx // 4, 5, 8, nz)] * 2 + [(3, nx // 32, ny, 128)] * 2 + [(len(LAYERS), ny, nz)] * 2
     scratch = [pltpu.SemaphoreType.DMA((nx // CHUNK, 3))]
     u, r, s, *sent = call(pack, [u.shape] * 3 + faces, raw, cells // 4, scratch, hbm_in=range(3))
     y = swap(sent[0:2], "gy")

time: 40.1 us -> 40.2 us (level)
  no operation moved by 1% of the time
where the time goes in v5:
time: 40.2 us; the launch traced here: 39.7 us
  starting transfers between devices  18.2 us (45%)
  Pallas kernels  16.5 us (41%)
  waiting for transfers between devices  4.81 us (12%)
    pallas_call x8, Pallas kernels, call(): pl.pallas_call(kernel, out_shape=[jax.ShapeDtypeStruct(s, F32) for s in o...  16.5 us
    ppermute x5, starting transfers between devices, swap(): return (lax.ppermute(sent[0], axis, near), got)  12.6 us
    ppermute x5, starting transfers between devices, swap(): got = lax.ppermute(sent[1], axis, far)  5.63 us
    ppermute x5, waiting for transfers between devices, swap(): got = lax.ppermute(sent[1], axis, far)  4.8 us
  transfers between devices with their start and end apart: 10, of which 2 were waited for; matrix products, arithmetic and copies ran while one was open for 0% of the time, Pallas kernels for 28%

profile of v5, /device:TPU:1, one launch (start us, length us, event | category | flops | bytes accessed | tf_op | source)
XLA Modules:
  0.0 39.7 jit_solution(12674114198924173253)
XLA Ops:
  0.0 3.2 %shard_map.37 = (f32[64,32,256]{2,1,0:T(8,128)S(1)}, f32[64,32,256]{2,1,0:T(8,128)S(1)}, f32[64,32,256]{2,1,0:T(8,128)S(1)}, f32[16,5,8,256]{3,2,1,0:T(8,128)S(1...) custom-call(f32[64,32,256]{2,1,0:T(8,128)} %u.1, ...), custom_call_target="tpu_custom_call" | custom-call | flops 131072 | bytes 1048576 | tf_op jit(solution)/shard_map/pallas_call | solution.py:20
  3.2 3.3 %collective-permute-start = (f32[16,5,8,256]{3,2,1,0:T(8,128)S(1)}, f32[16,5,8,256]{3,2,1,0:T(8,128)S(1)}, u32[]{:S(2)}, u32[]{:S(2)}) collective-permute-start(f32[16,5,8,256]{3,2,1,0:T(8,128)S(1)} %get-tuple-element.36), channel_id=1, source_target_pairs={{0,4},{4,0},{8,12},{12,8},{16,20},{20,16},{24,28},{28,24},{32,36},... | collective-permute-start | bytes 1966088 | tf_op jit(solution)/shard_map/ppermute | solution.py:41
  6.5 0.0 collective-permute-start.1
  6.5 1.1 %collective-permute-start.2 = (f32[3,2,32,128]{3,2,1,0:T(8,128)S(1)}, f32[3,2,32,128]{3,2,1,0:T(8,128)S(1)}, u32[]{:S(2)}, u32[]{:S(2)}) collective-permute-start(f32[3,2,32,128]{3,2,1,0:T(8,128)S(1)} %get-tuple-element.39), channel_id=1, source_target_pairs={{0,1},{1,0},{2,3},{3,2},{4,5},{5,4},{6,7},{7,6},{8,9},{9,8},{10,11... | collective-permute-start | bytes 294920 | tf_op jit(solution)/shard_map/ppermute | solution.py:41
  7.6 1.3 %collective-permute-start.6 = (f32[10,32,256]{2,1,0:T(8,128)S(1)}, f32[10,32,256]{2,1,0:T(8,128)S(1)}, u32[]{:S(2)}, u32[]{:S(2)}) collective-permute-start(f32[10,32,256]{2,1,0:T(8,128)S(1)} %get-tuple-element.61), channel_id=1, source_target_pairs={{0,64},{64,0},{128,192},{192,128},{1,65},{65,1},{129,193},{193,129... | collective-permute-start | bytes 983048 | tf_op jit(solution)/shard_map/ppermute | solution.py:41
  8.9 1.9 %collective-permute-start.7 = (f32[10,32,256]{2,1,0:T(8,128)S(1)}, f32[10,32,256]{2,1,0:T(8,128)S(1)}, u32[]{:S(2)}, u32[]{:S(2)}) collective-permute-start(f32[10,32,256]{2,1,0:T(8,128)S(1)} %get-tuple-element.62), channel_id=1, source_target_pairs={{0,192},{64,128},{128,64},{192,0},{1,193},{65,129},{129,65},{193,1... | collective-permute-start | bytes 983048 | tf_op jit(solution)/shard_map/ppermute | solution.py:40
  10.8 0.0 collective-permute-done.2.za
  10.8 1.8 %collective-permute-start.3 = (f32[3,2,32,128]{3,2,1,0:T(8,128)S(1)}, f32[3,2,32,128]{3,2,1,0:T(8,128)S(1)}, u32[]{:S(2)}, u32[]{:S(2)}) collective-permute-start(f32[3,2,32,128]{3,2,1,0:T(8,128)S(1)} %get-tuple-element.40), channel_id=1, source_target_pairs={{0,3},{1,2},{2,1},{3,0},{4,7},{5,6},{6,5},{7,4},{8,11},{9,10},{10,... | collective-permute-start | bytes 294920 | tf_op jit(solution)/shard_map/ppermute | solution.py:40
  12.6 3.2 %collective-permute-done.3.zb = f32[3,2,32,128]{3,2,1,0:T(8,128)S(1)} collective-permute-done((f32[3,2,32,128]{3,2,1,0:T(8,128)S(1)}, f32[3,2,32,128]{3,2,1,0:T(8,128)S(1)}, u32[]{:S(2)}, u32[]{:S(2)}) %collective-permute-start.3) | collective-permute-done | bytes 98336 | tf_op jit(solution)/shard_map/ppermute | solution.py:40
  15.8 6.1 %collective-permute-start.4 = (f32[3,2,8,128]{3,2,1,0:T(8,128)S(1)}, f32[3,2,8,128]{3,2,1,0:T(8,128)S(1)}, u32[]{:S(2)}, u32[]{:S(2)}) collective-permute-start(f32[3,2,8,128]{3,2,1,0:T(8,128)S(1)} %get-tuple-element.42), channel_id=1, source_target_pairs={{0,4},{4,0},{8,12},{12,8},{16,20},{20,16},{24,28},{28,24},{32,36},... | collective-permute-start | bytes 73736 | tf_op jit(solution)/shard_map/ppermute | solution.py:41
  21.9 0.0 collective-permute-done.near
  21.9 0.0 collective-permute-start.5
  21.9 1.2 %shard_map.39 = (f32[64,32,128]{2,1,0:T(8,128)S(1)}, f32[64,32,128]{2,1,0:T(8,128)S(1)}, f32[64,32,128]{2,1,0:T(8,128)S(1)}) custom-call(f32[3,2,32,128]{3,2,1,0:T(8,128)S(1)} %collective-permute-done.2.za, f32[3,2,32,128]{3,2,1,0:T(8,128)S(1)} %collective-permute-done.3.zb), custom_call_target="tpu_custom_call" | custom-call | flops 4194304 | bytes 1048576 | tf_op jit(solution)/shard_map/pallas_call | solution.py:20
  23.1 0.0 collective-permute-done.1.far
  23.1 0.4 shard_map.38
  23.5 0.0 collective-permute-done.4.b_near
  23.5 1.6 %collective-permute-done.5.b_far = f32[3,2,8,128]{3,2,1,0:T(8,128)S(1)} collective-permute-done((f32[3,2,8,128]{3,2,1,0:T(8,128)S(1)}, f32[3,2,8,128]{3,2,1,0:T(8,128)S(1)}, u32[]{:S(2)}, u32[]{:S(2)}) %collective-permute-start.5) | collective-permute-done | bytes 24608 | tf_op jit(solution)/shard_map/ppermute | solution.py:40
  25.2 0.4 %shard_map.41 = (f32[64,8,128]{2,1,0:T(8,128)S(1)}, f32[64,8,128]{2,1,0:T(8,128)S(1)}, f32[64,8,128]{2,1,0:T(8,128)S(1)}, f32[13,8,256]{2,1,0:T(8,128)S(1)}, f32[13,8,256]{2,1,0:T(8,128)S(1)}) custom-call(f32[3,2,8,128]{3,2,1,0:T(8,128)S(1)} %collective-permute-done.4.b_near, f32[3,2,8,128]{3,2,1,0:T(8,128)S(1)} %collective-permute-done.5.b_far, ...), custom_call_target="tpu_custom_call" | custom-call | flops 65536 | bytes 1048576 | tf_op jit(solution)/shard_map/pallas_call | solution.py:20
  25.6 0.7 %collective-permute-start.8 = (f32[13,8,256]{2,1,0:T(8,128)S(1)}, f32[13,8,256]{2,1,0:T(8,128)S(1)}, u32[]{:S(2)}, u32[]{:S(2)}) collective-permute-start(f32[13,8,256]{2,1,0:T(8,128)S(1)} %get-tuple-element.63), channel_id=1, source_target_pairs={{0,64},{64,0},{128,192},{192,128},{1,65},{65,1},{129,193},{193,129... | collective-permute-start | bytes 319496 | tf_op jit(solution)/shard_map/ppermute | solution.py:41
  26.3 1.9 %collective-permute-start.9 = (f32[13,8,256]{2,1,0:T(8,128)S(1)}, f32[13,8,256]{2,1,0:T(8,128)S(1)}, u32[]{:S(2)}, u32[]{:S(2)}) collective-permute-start(f32[13,8,256]{2,1,0:T(8,128)S(1)} %get-tuple-element.64), channel_id=1, source_target_pairs={{0,192},{64,128},{128,64},{192,0},{1,193},{65,129},{129,65},{193,1... | collective-permute-start | bytes 319496 | tf_op jit(solution)/shard_map/ppermute | solution.py:40
  28.2 1.9 %shard_map.42 = (f32[64,32,256]{2,1,0:T(8,128)S(1)}, f32[64,32,256]{2,1,0:T(8,128)S(1)}, f32[64,32,128]{2,1,0:T(8,128)S(1)}) custom-call(f32[64,32,256]{2,1,0:T(8,128)S(1)} %get-tuple-element.35.u.refs_0_, f32[64,32,256]{2,1,0:T(8,128)S(1)} %get-tuple-element.49.r.refs_4_, f32[64,32,256]{2,1,0:T(8,128)S(1)} %get-tuple-element.51.s), custom_call_target="tpu_custom_call" | custom-call | flops 10485760 | bytes 1048576 | tf_op jit(solution)/shard_map/pallas_call | solution.py:20
  30.1 7.4 %shard_map.43 = (f32[64,32,256]{2,1,0:T(8,128)}, f32[16,32,256]{2,1,0:T(8,128)S(1)}, f32[4,40,384]{2,1,0:T(8,128)S(1)}, f32[4,40,384]{2,1,0:T(8,128)S(1)}, f32[4,40,384]{2,1,0:T(8,128)S(1)}) custom-call(f32[64,32,256]{2,1,0:T(8,128)S(1)} %get-tuple-element.35.u.refs_0_, f32[64,8,256]{2,1,0:T(8,128)S(1)} %get-tuple-element.38.yu.refs_1_, ...), custom_call_target="tpu_custom_call" | custom-call | flops 31457280 | bytes 1048576 | tf_op jit(solution)/shard_map/pallas_call | solution.py:20
  37.5 0.0 collective-permute-done.6.refs_17_
  37.6 0.0 collective-permute-done.7.refs_18_
  37.6 0.0 collective-permute-done.8.refs_19_
  37.6 0.0 collective-permute-done.9.refs_20_
  37.6 2.0 %shard_map.44 = f32[64,32,256]{2,1,0:T(8,128)} custom-call(f32[64,32,256]{2,1,0:T(8,128)S(1)} %get-tuple-element.35.u.refs_0_, f32[64,8,256]{2,1,0:T(8,128)S(1)} %get-tuple-element.38.yu.refs_1_, f32[64,32,128]{2,1,0:T(8,128)S(1)} %get-tuple-element.41.tu.refs_2_, f32[64,8,128]{2,1,0:T(8,128)S(1)} %get-tuple-element.48.refs_3_, ...), custom_call_target="tpu_custom_call", output_to_operand_aliasing={{}: (12, {})} | custom-call | flops 4194304 | bytes 1048576 | tf_op jit(solution)/shard_map/pallas_call | solution.py:20
  (1 shorter events, 0.0 us)
Async XLA Ops:
  3.2 18.7 %collective-permute-start = (f32[16,5,8,256]{3,2,1,0:T(8,128)S(1)}, f32[16,5,8,256]{3,2,1,0:T(8,128)S(1)}, u32[]{:S(2)}, u32[]{:S(2)}) collective-permute-start(f32[16,5,8,256]{3,2,1,0:T(8,128)S(1)} %get-tuple-element.36), channel_id=1, source_target_pairs={{0,4},{4,0},{8,12},{12,8},{16,20},{20,16},{24,28},{28,24},{32,36},... | collective-permute-start | bytes 1966088 | tf_op jit(solution)/shard_map/ppermute | solution.py:41
  6.5 16.7 %collective-permute-start.1 = (f32[16,5,8,256]{3,2,1,0:T(8,128)S(1)}, f32[16,5,8,256]{3,2,1,0:T(8,128)S(1)}, u32[]{:S(2)}, u32[]{:S(2)}) collective-permute-start(f32[16,5,8,256]{3,2,1,0:T(8,128)S(1)} %get-tuple-element.37), channel_id=1, source_target_pairs={{0,60},{4,8},{8,4},{12,16},{16,12},{20,24},{24,20},{28,32},{32,28}... | collective-permute-start | bytes 1966088 | tf_op jit(solution)/shard_map/ppermute | solution.py:40
  6.5 4.3 %collective-permute-start.2 = (f32[3,2,32,128]{3,2,1,0:T(8,128)S(1)}, f32[3,2,32,128]{3,2,1,0:T(8,128)S(1)}, u32[]{:S(2)}, u32[]{:S(2)}) collective-permute-start(f32[3,2,32,128]{3,2,1,0:T(8,128)S(1)} %get-tuple-element.39), channel_id=1, source_target_pairs={{0,1},{1,0},{2,3},{3,2},{4,5},{5,4},{6,7},{7,6},{8,9},{9,8},{10,11... | collective-permute-start | bytes 294920 | tf_op jit(solution)/shard_map/ppermute | solution.py:41
  7.6 30.0 %collective-permute-start.6 = (f32[10,32,256]{2,1,0:T(8,128)S(1)}, f32[10,32,256]{2,1,0:T(8,128)S(1)}, u32[]{:S(2)}, u32[]{:S(2)}) collective-permute-start(f32[10,32,256]{2,1,0:T(8,128)S(1)} %get-tuple-element.61), channel_id=1, source_target_pairs={{0,64},{64,0},{128,192},{192,128},{1,65},{65,1},{129,193},{193,129... | collective-permute-start | bytes 983048 | tf_op jit(solution)/shard_map/ppermute | solution.py:41
  8.9 28.7 %collective-permute-start.7 = (f32[10,32,256]{2,1,0:T(8,128)S(1)}, f32[10,32,256]{2,1,0:T(8,128)S(1)}, u32[]{:S(2)}, u32[]{:S(2)}) collective-permute-start(f32[10,32,256]{2,1,0:T(8,128)S(1)} %get-tuple-element.62), channel_id=1, source_target_pairs={{0,192},{64,128},{128,64},{192,0},{1,193},{65,129},{129,65},{193,1... | collective-permute-start | bytes 983048 | tf_op jit(solution)/shard_map/ppermute | solution.py:40
  10.8 5.0 %collective-permute-start.3 = (f32[3,2,32,128]{3,2,1,0:T(8,128)S(1)}, f32[3,2,32,128]{3,2,1,0:T(8,128)S(1)}, u32[]{:S(2)}, u32[]{:S(2)}) collective-permute-start(f32[3,2,32,128]{3,2,1,0:T(8,128)S(1)} %get-tuple-element.40), channel_id=1, source_target_pairs={{0,3},{1,2},{2,1},{3,0},{4,7},{5,6},{6,5},{7,4},{8,11},{9,10},{10,... | collective-permute-start | bytes 294920 | tf_op jit(solution)/shard_map/ppermute | solution.py:40
  15.8 7.7 %collective-permute-start.4 = (f32[3,2,8,128]{3,2,1,0:T(8,128)S(1)}, f32[3,2,8,128]{3,2,1,0:T(8,128)S(1)}, u32[]{:S(2)}, u32[]{:S(2)}) collective-permute-start(f32[3,2,8,128]{3,2,1,0:T(8,128)S(1)} %get-tuple-element.42), channel_id=1, source_target_pairs={{0,4},{4,0},{8,12},{12,8},{16,20},{20,16},{24,28},{28,24},{32,36},... | collective-permute-start | bytes 73736 | tf_op jit(solution)/shard_map/ppermute | solution.py:41
  21.9 3.3 %collective-permute-start.5 = (f32[3,2,8,128]{3,2,1,0:T(8,128)S(1)}, f32[3,2,8,128]{3,2,1,0:T(8,128)S(1)}, u32[]{:S(2)}, u32[]{:S(2)}) collective-permute-start(f32[3,2,8,128]{3,2,1,0:T(8,128)S(1)} %get-tuple-element.43), channel_id=1, source_target_pairs={{0,60},{4,8},{8,4},{12,16},{16,12},{20,24},{24,20},{28,32},{32,28}... | collective-permute-start | bytes 73736 | tf_op jit(solution)/shard_map/ppermute | solution.py:40
  25.6 12.0 %collective-permute-start.8 = (f32[13,8,256]{2,1,0:T(8,128)S(1)}, f32[13,8,256]{2,1,0:T(8,128)S(1)}, u32[]{:S(2)}, u32[]{:S(2)}) collective-permute-start(f32[13,8,256]{2,1,0:T(8,128)S(1)} %get-tuple-element.63), channel_id=1, source_target_pairs={{0,64},{64,0},{128,192},{192,128},{1,65},{65,1},{129,193},{193,129... | collective-permute-start | bytes 319496 | tf_op jit(solution)/shard_map/ppermute | solution.py:41
  26.3 11.2 %collective-permute-start.9 = (f32[13,8,256]{2,1,0:T(8,128)S(1)}, f32[13,8,256]{2,1,0:T(8,128)S(1)}, u32[]{:S(2)}, u32[]{:S(2)}) collective-permute-start(f32[13,8,256]{2,1,0:T(8,128)S(1)} %get-tuple-element.64), channel_id=1, source_target_pairs={{0,192},{64,128},{128,64},{192,0},{1,193},{65,129},{129,65},{193,1... | collective-permute-start | bytes 319496 | tf_op jit(solution)/shard_map/ppermute | solution.py:40
